TPU v7x, 32 devices: a whole 2x2x4 slice. The times are simulated.
32 devices in a mesh: fsdp: 2 (over core), ctx: 4 (over y, x), tensor: 4 (over z).
Axes of the slice: x: 2, y: 2, z: 4, core: 2. Of those that a mesh axis runs over, the one named last changes fastest.
Arguments:
- tokens: bfloat16 [4, 1024, 2048], P('fsdp', ('ctx', 'tensor')), may hold values from -6 to 6
- segments: int32 [4, 1024], P('fsdp'), may hold values from 0 to 6, as said below
- positions: int32 [4, 1024], P('fsdp'), may hold values from 0 to 1226, as said below
- query_weight: bfloat16 [2048, 2048], P(('fsdp', 'ctx'), 'tensor'), may hold values from -0.125 to 0.125
- key_weight: bfloat16 [2048, 2048], P(('fsdp', 'ctx'), 'tensor'), may hold values from -0.125 to 0.125
- value_weight: bfloat16 [2048, 2048], P(('fsdp', 'ctx'), 'tensor'), may hold values from -0.125 to 0.125
- output_weight: bfloat16 [2048, 2048], P(('fsdp', 'ctx'), 'tensor'), may hold values from -0.125 to 0.125
- gate_weight: bfloat16 [2048, 8192], P(('fsdp', 'ctx'), 'tensor'), may hold values from -0.125 to 0.125
- up_projection_weight: bfloat16 [2048, 8192], P(('fsdp', 'ctx'), 'tensor'), may hold values from -0.125 to 0.125
- down_weight: bfloat16 [2048, 8192], P(('fsdp', 'ctx'), 'tensor'), may hold values from -0.0625 to 0.0625
- query_gain: float32 [2048], replicated, may hold values from 0.5 to 1.5
- key_gain: float32 [2048], replicated, may hold values from 0.5 to 1.5
- attention_gain: float32 [2048], replicated, may hold values from 0.5 to 1.5
- feedforward_gain: float32 [2048], replicated, may hold values from 0.5 to 1.5
- cotangent: bfloat16 [4, 1024, 2048], P('fsdp', ('ctx', 'tensor')), may hold values from -6 to 6
Outputs:
- block_out: bfloat16 [4, 1024, 2048], P('fsdp', ('ctx', 'tensor'))
- input_grad: float32 [4, 1024, 2048], P('fsdp', ('ctx', 'tensor'))
- query_weight_grad: float32 [2048, 2048], P(('fsdp', 'ctx'), 'tensor')
- key_weight_grad: float32 [2048, 2048], P(('fsdp', 'ctx'), 'tensor')
- value_weight_grad: float32 [2048, 2048], P(('fsdp', 'ctx'), 'tensor')
- output_weight_grad: float32 [2048, 2048], P(('fsdp', 'ctx'), 'tensor')
- gate_weight_grad: float32 [2048, 8192], P(('fsdp', 'ctx'), 'tensor')
- up_weight_grad: float32 [2048, 8192], P(('fsdp', 'ctx'), 'tensor')
- down_weight_grad: float32 [2048, 8192], P(('fsdp', 'ctx'), 'tensor')
- query_gain_grad: float32 [2048], replicated
- key_gain_grad: float32 [2048], replicated
- attention_gain_grad: float32 [2048], replicated
- feedforward_gain_grad: float32 [2048], replicated
Inputs may be any that keep to these rules, and one draw needn't show every extreme that they name: `segments`: in each sequence the numbers start at 0 and rise by one where a new document begins; documents hold a fifth of 1024 (rounded down) to 2047 tokens, and the first may have begun before the sequence. `positions`: each token's index in its document; it rises by one from token to token within a document and is 0 where a document begins inside the sequence.
All inputs are finite; a program needn't handle non-finite values.
Results may differ from a plain program's by a relative error of at most 0.017.
Values may be sent and summed in bfloat16 or wider, within the bound.
A program may use at most 256 MiB of HBM per device.

v0:
```python
import jax
import jax.numpy as jnp
from jax import lax
from jax.sharding import PartitionSpec as P

D = 2048
HD = 128


epsilon = 1e-06
rope_theta = 500000.0
masked_score = -1e30


def rope_tables(position_ids):
    freq_index = jnp.arange(HD // 2, dtype=jnp.float32)
    inverse = rope_theta ** (-2.0 * freq_index / HD)
    angles = position_ids.astype(jnp.float32)[..., None] * inverse
    return (jnp.cos(angles), jnp.sin(angles))


def rotate(values, cosine, sine):
    half = values.shape[-1] // 2
    first_half = values[..., :half]
    second_half = values[..., half:]
    cos_wide = cosine[..., None, :]
    sin_wide = sine[..., None, :]
    return jnp.concatenate(
        [
            first_half * cos_wide - second_half * sin_wide,
            second_half * cos_wide + first_half * sin_wide,
        ],
        axis=-1,
    )


def unrotate(values, cosine, sine):
    half = values.shape[-1] // 2
    first_half = values[..., :half]
    second_half = values[..., half:]
    cos_wide = cosine[..., None, :]
    sin_wide = sine[..., None, :]
    return jnp.concatenate(
        [
            first_half * cos_wide + second_half * sin_wide,
            second_half * cos_wide - first_half * sin_wide,
        ],
        axis=-1,
    )


def root_mean_square_scale(values):
    return lax.rsqrt(jnp.mean(values * values, axis=-1, keepdims=True) + epsilon)


def norm_back(grad_unit, unit, scale):
    return scale * (grad_unit - unit * jnp.mean(grad_unit * unit, axis=-1, keepdims=True))


def project(matrix_rows, weight_matrix):
    return jnp.einsum("xmj,je->xme", matrix_rows, weight_matrix, preferred_element_type=jnp.float32)


def project_back(matrix_rows, weight_matrix):
    return jnp.einsum("rhy,iy->rhi", matrix_rows, weight_matrix, preferred_element_type=jnp.float32)


def weight_term(left_operand_rows, right_operand_rows):
    return jnp.einsum(
        "prt,pre->te", left_operand_rows, right_operand_rows, preferred_element_type=jnp.float32
    )


def gather_tokens(matrix_rows):
    return lax.all_gather(matrix_rows, "tensor", axis=1, tiled=True)


def sum_tokens(terms):
    return lax.psum_scatter(terms, "tensor", scatter_dimension=1, tiled=True)


def body(
    tokens,
    segments,
    positions,
    query_weight,
    key_weight,
    value_weight,
    output_weight,
    gate_weight,
    up_projection_weight,
    down_weight,
    query_gain,
    key_gain,
    attention_gain,
    feedforward_gain,
    cotangent,
):
    ctx_index = lax.axis_index("ctx")
    tensor_index = lax.axis_index("tensor")
    gathered = (
        lax.all_gather(query_weight, ("fsdp", "ctx"), axis=0, tiled=True),
        lax.all_gather(key_weight, ("fsdp", "ctx"), axis=0, tiled=True),
        lax.all_gather(value_weight, ("fsdp", "ctx"), axis=0, tiled=True),
        lax.all_gather(output_weight, ("fsdp", "ctx"), axis=0, tiled=True),
        lax.all_gather(gate_weight, ("fsdp", "ctx"), axis=0, tiled=True),
        lax.all_gather(up_projection_weight, ("fsdp", "ctx"), axis=0, tiled=True),
        lax.all_gather(down_weight, ("fsdp", "ctx"), axis=0, tiled=True),
    )
    query_full, key_full, value_full, output_full, gate_full, up_full, down_full = gathered
    width_local = query_full.shape[1]
    heads_local = width_local // HD
    gain_start = tensor_index * width_local
    query_gain_local = lax.dynamic_slice_in_dim(query_gain, gain_start, width_local)
    key_gain_local = lax.dynamic_slice_in_dim(key_gain, gain_start, width_local)
    score_scale = HD ** (-0.5)
    tokens_block = gather_tokens(tokens)
    seq_count = tokens_block.shape[0]
    block_len = tokens_block.shape[1]
    full_len = segments.shape[1]
    query_lin = project(tokens_block, query_full)
    key_lin = project(tokens_block, key_full)
    value_lin = project(tokens_block, value_full)
    query_squared, key_sq = lax.psum(
        (jnp.sum(query_lin * query_lin, axis=-1), jnp.sum(key_lin * key_lin, axis=-1)), "tensor"
    )
    query_scale = lax.rsqrt(query_squared / D + epsilon)[..., None]
    key_scale = lax.rsqrt(key_sq / D + epsilon)[..., None]
    query_unit = query_lin * query_scale
    key_unit = key_lin * key_scale
    block_pos = lax.dynamic_slice_in_dim(positions, ctx_index * block_len, block_len, 1)
    cosine, sine = rope_tables(block_pos)

    def heads_of(values):
        return values.reshape(seq_count, block_len, heads_local, HD)

    query_rot = rotate(heads_of(query_unit * query_gain_local), cosine, sine).astype(jnp.bfloat16)
    key_rot = rotate(heads_of(key_unit * key_gain_local), cosine, sine).astype(jnp.bfloat16)
    value_rot = heads_of(value_lin).astype(jnp.bfloat16)
    query_heads, key_heads, value_heads = (
        lax.all_to_all(query_rot, "ctx", split_axis=2, concat_axis=1, tiled=True),
        lax.all_to_all(key_rot, "ctx", split_axis=2, concat_axis=1, tiled=True),
        lax.all_to_all(value_rot, "ctx", split_axis=2, concat_axis=1, tiled=True),
    )
    token_index = jnp.arange(full_len, dtype=jnp.int32)
    allowed = (segments[:, :, None] == segments[:, None, :]) & (
        token_index[None, :, None] >= token_index[None, None, :]
    )
    allowed = allowed[:, None]

    def masked_scores():
        raw_scores = (
            jnp.einsum(
                "sqhd,skhd->shqk", query_heads, key_heads, preferred_element_type=jnp.float32
            )
            * score_scale
        )
        return jnp.where(allowed, raw_scores, masked_score)

    scores = masked_scores()
    top_score = jnp.max(scores, axis=-1, keepdims=True)
    log_total = top_score + jnp.log(jnp.sum(jnp.exp(scores - top_score), axis=-1, keepdims=True))
    probs_b = jnp.exp(scores - log_total).astype(jnp.bfloat16)
    attended = jnp.einsum(
        "shqk,skhd->sqhd", probs_b, value_heads, preferred_element_type=jnp.float32
    ).astype(jnp.bfloat16)
    attended_block = lax.all_to_all(
        attended, "ctx", split_axis=1, concat_axis=2, tiled=True
    ).reshape(seq_count, block_len, width_local)
    attention_out = sum_tokens(project_back(attended_block, output_full))
    attention_scale = root_mean_square_scale(attention_out)
    attention_unit = attention_out * attention_scale
    hidden_state = tokens.astype(jnp.float32) + attention_unit * attention_gain
    hidden_block = gather_tokens(hidden_state.astype(jnp.bfloat16))
    gate_lin = project(hidden_block, gate_full)
    up_lin = project(hidden_block, up_full)
    gate_sig = jax.nn.sigmoid(gate_lin)
    gate_act = gate_lin * gate_sig
    mixed = (gate_act * up_lin).astype(jnp.bfloat16)
    mixed_out = sum_tokens(project_back(mixed, down_full))
    mixed_scale = root_mean_square_scale(mixed_out)
    mixed_unit = mixed_out * mixed_scale
    block_out = (hidden_state + mixed_unit * feedforward_gain).astype(jnp.bfloat16)
    back_weights = (
        lax.all_gather(query_weight, ("fsdp", "ctx"), axis=0, tiled=True),
        lax.all_gather(key_weight, ("fsdp", "ctx"), axis=0, tiled=True),
        lax.all_gather(value_weight, ("fsdp", "ctx"), axis=0, tiled=True),
        lax.all_gather(output_weight, ("fsdp", "ctx"), axis=0, tiled=True),
        lax.all_gather(gate_weight, ("fsdp", "ctx"), axis=0, tiled=True),
        lax.all_gather(up_projection_weight, ("fsdp", "ctx"), axis=0, tiled=True),
        lax.all_gather(down_weight, ("fsdp", "ctx"), axis=0, tiled=True),
    )
    query_back, key_back, value_back, output_back, gate_back, up_back, down_back = back_weights
    upstream = cotangent.astype(jnp.float32)
    ffn_gain_grad = jnp.sum(upstream * mixed_unit, axis=(0, 1))
    mixed_grad = norm_back(upstream * feedforward_gain, mixed_unit, mixed_scale).astype(
        jnp.bfloat16
    )
    mixed_grad_block = gather_tokens(mixed_grad)
    inner_grad = project(mixed_grad_block, down_back)
    down_wgrad = weight_term(mixed_grad_block, mixed)
    gate_lin_grad = (inner_grad * up_lin * gate_sig * (1.0 + gate_lin * (1.0 - gate_sig))).astype(
        jnp.bfloat16
    )
    up_lin_grad = (inner_grad * gate_act).astype(jnp.bfloat16)
    gate_wgrad = weight_term(hidden_block, gate_lin_grad)
    up_wgrad = weight_term(hidden_block, up_lin_grad)
    hidden_grad = upstream + sum_tokens(
        project_back(gate_lin_grad, gate_back) + project_back(up_lin_grad, up_back)
    )
    attn_gain_grad = jnp.sum(hidden_grad * attention_unit, axis=(0, 1))
    attention_grad = norm_back(
        hidden_grad * attention_gain, attention_unit, attention_scale
    ).astype(jnp.bfloat16)
    attention_grad_block = gather_tokens(attention_grad)
    attended_output_gradient = project(attention_grad_block, output_back).astype(jnp.bfloat16)
    output_wgrad = weight_term(attention_grad_block, attended_block)
    attended_grad_heads = lax.all_to_all(
        heads_of(attended_output_gradient), "ctx", split_axis=2, concat_axis=1, tiled=True
    )
    probs_full = jnp.exp(masked_scores() - log_total)
    probs_again = probs_full.astype(jnp.bfloat16)
    value_grad_heads = jnp.einsum(
        "shqk,sqhd->skhd", probs_again, attended_grad_heads, preferred_element_type=jnp.float32
    ).astype(jnp.bfloat16)
    prob_grad = jnp.einsum(
        "sqhd,skhd->shqk", attended_grad_heads, value_heads, preferred_element_type=jnp.float32
    )
    delta_rows = jnp.einsum(
        "sqhd,sqhd->shq", attended_grad_heads, attended, preferred_element_type=jnp.float32
    )
    score_grad = (probs_full * (prob_grad - delta_rows[..., None])).astype(jnp.bfloat16)
    query_grad_heads = (
        jnp.einsum("shqk,skhd->sqhd", score_grad, key_heads, preferred_element_type=jnp.float32)
        * score_scale
    ).astype(jnp.bfloat16)
    key_grad_heads = (
        jnp.einsum("shqk,sqhd->skhd", score_grad, query_heads, preferred_element_type=jnp.float32)
        * score_scale
    ).astype(jnp.bfloat16)
    query_grad_rot, key_grad_rot, value_grad_rot = (
        lax.all_to_all(query_grad_heads, "ctx", split_axis=1, concat_axis=2, tiled=True),
        lax.all_to_all(key_grad_heads, "ctx", split_axis=1, concat_axis=2, tiled=True),
        lax.all_to_all(value_grad_heads, "ctx", split_axis=1, concat_axis=2, tiled=True),
    )
    query_grad_n = unrotate(query_grad_rot.astype(jnp.float32), cosine, sine).reshape(
        seq_count, block_len, width_local
    )
    key_grad_n = unrotate(key_grad_rot.astype(jnp.float32), cosine, sine).reshape(
        seq_count, block_len, width_local
    )
    query_gain_part = jnp.sum(query_grad_n * query_unit, axis=(0, 1))
    key_gain_part = jnp.sum(key_grad_n * key_unit, axis=(0, 1))
    query_grad_u = query_grad_n * query_gain_local
    key_grad_u = key_grad_n * key_gain_local
    query_inner, key_inner = lax.psum(
        (jnp.sum(query_grad_u * query_unit, axis=-1), jnp.sum(key_grad_u * key_unit, axis=-1)),
        "tensor",
    )
    query_pre = (query_scale * (query_grad_u - query_unit * (query_inner / D)[..., None])).astype(
        jnp.bfloat16
    )
    key_pre = (key_scale * (key_grad_u - key_unit * (key_inner / D)[..., None])).astype(
        jnp.bfloat16
    )
    value_pre = value_grad_rot.reshape(seq_count, block_len, width_local)
    input_attn = sum_tokens(
        project_back(query_pre, query_back)
        + project_back(key_pre, key_back)
        + project_back(value_pre, value_back)
    )
    input_grad = hidden_grad + input_attn
    query_wgrad = weight_term(tokens_block, query_pre)
    key_wgrad = weight_term(tokens_block, key_pre)
    value_wgrad = weight_term(tokens_block, value_pre)
    query_gain_full = lax.dynamic_update_slice_in_dim(
        jnp.zeros((D,), jnp.float32), query_gain_part, gain_start, 0
    )
    key_gain_full = lax.dynamic_update_slice_in_dim(
        jnp.zeros((D,), jnp.float32), key_gain_part, gain_start, 0
    )
    query_gain_grad, key_gain_grad, attention_gain_grad, feedforward_gain_grad = lax.psum(
        (query_gain_full, key_gain_full, attn_gain_grad, ffn_gain_grad), ("fsdp", "ctx", "tensor")
    )
    (
        query_reduced,
        key_reduced,
        value_reduced,
        output_reduced,
        gate_reduced,
        up_reduced,
        down_reduced,
    ) = (
        lax.psum_scatter(query_wgrad, ("fsdp", "ctx"), scatter_dimension=0, tiled=True),
        lax.psum_scatter(key_wgrad, ("fsdp", "ctx"), scatter_dimension=0, tiled=True),
        lax.psum_scatter(value_wgrad, ("fsdp", "ctx"), scatter_dimension=0, tiled=True),
        lax.psum_scatter(output_wgrad, ("fsdp", "ctx"), scatter_dimension=0, tiled=True),
        lax.psum_scatter(gate_wgrad, ("fsdp", "ctx"), scatter_dimension=0, tiled=True),
        lax.psum_scatter(up_wgrad, ("fsdp", "ctx"), scatter_dimension=0, tiled=True),
        lax.psum_scatter(down_wgrad, ("fsdp", "ctx"), scatter_dimension=0, tiled=True),
    )
    return (
        block_out,
        input_grad,
        query_reduced,
        key_reduced,
        value_reduced,
        output_reduced,
        gate_reduced,
        up_reduced,
        down_reduced,
        query_gain_grad,
        key_gain_grad,
        attention_gain_grad,
        feedforward_gain_grad,
    )


def solution(mesh):
    in_specs = (
        P("fsdp", ("ctx", "tensor"), None),
        P("fsdp", None),
        P("fsdp", None),
        P(("fsdp", "ctx"), "tensor"),
        P(("fsdp", "ctx"), "tensor"),
        P(("fsdp", "ctx"), "tensor"),
        P(("fsdp", "ctx"), "tensor"),
        P(("fsdp", "ctx"), "tensor"),
        P(("fsdp", "ctx"), "tensor"),
        P(("fsdp", "ctx"), "tensor"),
        P(),
        P(),
        P(),
        P(),
        P("fsdp", ("ctx", "tensor"), None),
    )
    out_specs = (
        P("fsdp", ("ctx", "tensor"), None),
        P("fsdp", ("ctx", "tensor"), None),
        P(("fsdp", "ctx"), "tensor"),
        P(("fsdp", "ctx"), "tensor"),
        P(("fsdp", "ctx"), "tensor"),
        P(("fsdp", "ctx"), "tensor"),
        P(("fsdp", "ctx"), "tensor"),
        P(("fsdp", "ctx"), "tensor"),
        P(("fsdp", "ctx"), "tensor"),
        P(),
        P(),
        P(),
        P(),
    )
    return jax.shard_map(body, mesh=mesh, in_specs=in_specs, out_specs=out_specs, check_vma=False)
```

profile of v0, /device:TPU:0, one launch (start us, length us, event | category | flops | bytes accessed | tf_op | source)
XLA Modules:
  0.0 1508.3 jit_solution(17496973479163622820)
XLA Ops:
  14.5 43.4 %all-gather.12.cloned.1.call-done = bf16[2,256,2048]{2,1,0:T(8,128)(2,1)} async-done(((bf16[2,64,2048]{2,1,0:T(8,128)(2,1)}), bf16[2,256,2048]{2,1,0:T(8,128)(2,1)}) %all-gather.12.cloned.1.call-update) | async-done | bytes 2097168 | tf_op jit(solution)/shard_map/all_gather | solution.py:75
  58.0 28.5 %all-gather.16.cloned.1.call-done = bf16[2048,512]{1,0:T(8,128)(2,1)} async-done(((bf16[256,512]{1,0:T(8,128)(2,1)}), bf16[2048,512]{1,0:T(8,128)(2,1)}) %all-gather.16.cloned.1.call-update) | async-done | bytes 2097168 | tf_op jit(solution)/shard_map/all_gather | solution.py:102
  86.5 3.5 multiply_reduce_fusion.8
  90.0 26.1 %all-gather.18.cloned.1.call-done = bf16[2048,512]{1,0:T(8,128)(2,1)} async-done(((bf16[256,512]{1,0:T(8,128)(2,1)}), bf16[2048,512]{1,0:T(8,128)(2,1)}) %all-gather.18.cloned.1.call-update) | async-done | bytes 2097168 | tf_op jit(solution)/shard_map/all_gather | solution.py:103
  116.2 3.8 multiply_reduce_fusion.7
  120.0 11.7 all-reduce.2
  132.8 2.5 reshape.204
  135.3 3.9 fusion.62
  146.0 3.5 all-to-all-start.2
  151.6 4.4 all-to-all-done.2
  156.0 3.5 all-to-all-start.1
  159.5 2.8 fusion.47
  163.3 2.8 all-to-all-done.1
  166.1 4.1 all-to-all-start
  174.0 7.8 all-to-all-done
  185.3 4.0 fusion.63
  195.3 10.6 all_to_all.108
  209.1 4.8 fusion.19
  214.8 75.6 %reduce-scatter.12.cloned.1.call-done = f32[2,64,2048]{2,1,0:T(8,128)} async-done(((f32[2,256,2048]{2,1,0:T(8,128)}), f32[2,64,2048]{2,1,0:T(8,128)}) %reduce-scatter.12.cloned.1.call-update) | async-done | bytes 1048592 | tf_op jit(solution)/shard_map/reduce_scatter | solution.py:79
  295.9 51.1 %all-gather.24.cloned.1.call-done = bf16[2048,2048]{1,0:T(8,128)(2,1)} async-done(((bf16[256,2048]{1,0:T(8,128)(2,1)}), bf16[2048,2048]{1,0:T(8,128)(2,1)}) %all-gather.24.cloned.1.call-update) | async-done | bytes 8388624 | tf_op jit(solution)/shard_map/all_gather | solution.py:106
  347.0 47.8 %all-gather.22.cloned.1.call-done = bf16[2,256,2048]{2,1,0:T(8,128)(2,1)} async-done(((bf16[2,64,2048]{2,1,0:T(8,128)(2,1)}), bf16[2,256,2048]{2,1,0:T(8,128)(2,1)}) %all-gather.22.cloned.1.call-update) | async-done | bytes 2097168 | tf_op jit(solution)/shard_map/all_gather | solution.py:75
  394.8 10.6 fusion.10
  405.4 44.4 %all-gather.26.cloned.1.call-done = bf16[2048,2048]{1,0:T(8,128)(2,1)} async-done(((bf16[256,2048]{1,0:T(8,128)(2,1)}), bf16[2048,2048]{1,0:T(8,128)(2,1)}) %all-gather.26.cloned.1.call-update) | async-done | bytes 8388624 | tf_op jit(solution)/shard_map/all_gather | solution.py:107
  449.8 12.5 multiply_convert_fusion.3
  462.3 43.5 %all-gather.28.cloned.1.call-done = bf16[2048,2048]{1,0:T(8,128)(2,1)} async-done(((bf16[256,2048]{1,0:T(8,128)(2,1)}), bf16[2048,2048]{1,0:T(8,128)(2,1)}) %all-gather.28.cloned.1.call-update) | async-done | bytes 8388624 | tf_op jit(solution)/shard_map/all_gather | solution.py:108
  505.8 10.5 fusion.2
  516.5 76.9 %reduce-scatter.14.cloned.1.call-done = f32[2,64,2048]{2,1,0:T(8,128)} async-done(((f32[2,256,2048]{2,1,0:T(8,128)}), f32[2,64,2048]{2,1,0:T(8,128)}) %reduce-scatter.14.cloned.1.call-update) | async-done | bytes 1048592 | tf_op jit(solution)/shard_map/reduce_scatter | solution.py:79
  596.4 2.3 fusion.55
  598.9 46.1 %all-gather.30.cloned.1.call-done = bf16[2,256,2048]{2,1,0:T(8,128)(2,1)} async-done(((bf16[2,64,2048]{2,1,0:T(8,128)(2,1)}), bf16[2,256,2048]{2,1,0:T(8,128)(2,1)}) %all-gather.30.cloned.1.call-update) | async-done | bytes 2097168 | tf_op jit(solution)/shard_map/all_gather | solution.py:75
  645.0 11.9 multiply_convert_fusion.2
  656.9 8.5 fusion.4
  665.4 9.5 fusion.14
  675.0 75.7 %reduce-scatter.16.cloned.1.call-done = f32[2,64,2048]{2,1,0:T(8,128)} async-done(((f32[2,256,2048]{2,1,0:T(8,128)}), f32[2,64,2048]{2,1,0:T(8,128)}) %reduce-scatter.16.cloned.1.call-update) | async-done | bytes 1048592 | tf_op jit(solution)/shard_map/reduce_scatter | solution.py:79
  752.8 3.3 multiply_convert_fusion.6
  756.2 46.3 %all-gather.32.cloned.1.call-done = bf16[2,256,2048]{2,1,0:T(8,128)(2,1)} async-done(((bf16[2,64,2048]{2,1,0:T(8,128)(2,1)}), bf16[2,256,2048]{2,1,0:T(8,128)(2,1)}) %all-gather.32.cloned.1.call-update) | async-done | bytes 2097168 | tf_op jit(solution)/shard_map/all_gather | solution.py:75
  802.4 3.5 fusion.44
  806.0 11.8 all_to_all.109
  817.9 5.7 fusion.50
  824.9 9.8 all_to_all.110
  837.9 3.3 convolution_bitcast_fusion.4
  843.9 6.0 multiply_convert_fusion
  853.8 4.1 all-to-all-start.5
  857.9 3.7 fusion.42
  862.7 4.1 all-to-all-done.5
  866.9 4.2 all-to-all-start.6
  872.2 9.2 all-to-all-done.6
  886.2 10.2 all-reduce.1
  896.3 2.4 multiply_convert_fusion.4
  899.5 3.3 convolution_bitcast_fusion.5
  905.7 3.3 convolution_bitcast_fusion.6
  909.5 3.2 fusion.21
  914.6 3.4 add_add_fusion
  919.0 4.9 convolution_bitcast_fusion.3
  923.9 12.6 convolution_bitcast_fusion
  938.1 9.8 convolution_bitcast_fusion.2
  948.2 9.8 convolution_bitcast_fusion.1
  958.5 39.2 %all-reduce = (f32[2048]{0:T(1024)}, f32[2048]{0:T(1024)}, f32[2048]{0:T(1024)}, f32[2048]{0:T(1024)}) all-reduce(f32[2048]{0:T(1024)S(1)} %dynamic_update_slice.6, f32[2048]{0:T(1024)S(1)} %dynamic_update_slice.7, f32[2048]{0:T(1024)S(1)} %get-tuple-element.52, ...), channel_id=1, replica_groups=mesh['fsdp'=2,'ctx'=4,'tensor'=4] {'fsdp','ctx','tensor'}, use_global_device_ids=true, to_apply=%region_26.27 | all-reduce | flops 8192 | bytes 65536 | tf_op jit(solution)/shard_map/psum | solution.py:282
  1001.8 3.9 reduce-scatter.20.cloned.1.call-done
  1007.8 76.9 %reduce-scatter.18.cloned.1.call-done = f32[2,64,2048]{2,1,0:T(8,128)} async-done(((f32[2,256,2048]{2,1,0:T(8,128)}), f32[2,64,2048]{2,1,0:T(8,128)}) %reduce-scatter.18.cloned.1.call-update) | async-done | bytes 1048592 | tf_op jit(solution)/shard_map/reduce_scatter | solution.py:79
  1084.7 2.4 fusion.60
  1087.1 53.2 %reduce-scatter.26.cloned.1.call-done = f32[256,512]{1,0:T(8,128)} async-done(((f32[2048,512]{1,0:T(8,128)}), f32[256,512]{1,0:T(8,128)}) %reduce-scatter.26.cloned.1.call-update) | async-done | bytes 524304 | tf_op jit(solution)/shard_map/reduce_scatter | solution.py:297
  1140.3 120.2 %reduce-scatter.32.cloned.1.call-done = f32[256,2048]{1,0:T(8,128)} async-done(((f32[2048,2048]{1,0:T(8,128)}), f32[256,2048]{1,0:T(8,128)}) %reduce-scatter.32.cloned.1.call-update) | async-done | bytes 2097168 | tf_op jit(solution)/shard_map/reduce_scatter | solution.py:300
  1260.5 120.4 %reduce-scatter.28.cloned.1.call-done = f32[256,2048]{1,0:T(8,128)} async-done(((f32[2048,2048]{1,0:T(8,128)}), f32[256,2048]{1,0:T(8,128)}) %reduce-scatter.28.cloned.1.call-update) | async-done | bytes 2097168 | tf_op jit(solution)/shard_map/reduce_scatter | solution.py:298
  1380.9 120.4 %reduce-scatter.30.cloned.1.call-done = f32[256,2048]{1,0:T(8,128)} async-done(((f32[2048,2048]{1,0:T(8,128)}), f32[256,2048]{1,0:T(8,128)}) %reduce-scatter.30.cloned.1.call-update) | async-done | bytes 2097168 | tf_op jit(solution)/shard_map/reduce_scatter | solution.py:299
  (194 shorter events, 80.1 us)
Async XLA Ops:
  7.2 50.8 %all-gather.12.cloned.1.call-start = ((), (), s32[]{:S(2)}) async-start(), calls=%async_computation.19 | async-start | bytes 2621440 | tf_op jit(solution)/shard_map/all_gather | solution.py:75
  7.9 78.6 %all-gather.16.cloned.1.call-start = ((), (), s32[]{:S(2)}) async-start(), calls=%async_computation.21 | async-start | bytes 2359296 | tf_op jit(solution)/shard_map/all_gather | solution.py:102
  8.7 107.5 %all-gather.18.cloned.1.call-start = ((), (), s32[]{:S(2)}) async-start(), calls=%async_computation.22 | async-start | bytes 2359296 | tf_op jit(solution)/shard_map/all_gather | solution.py:103
  9.4 150.1 %all-gather.14.cloned.1.call-start = ((), (), s32[]{:S(2)}) async-start(), calls=%async_computation.20 | async-start | bytes 2359296 | tf_op jit(solution)/shard_map/all_gather | solution.py:104
  10.0 198.3 %all-gather.20.cloned.1.call-start = ((), (), s32[]{:S(2)}) async-start(), calls=%async_computation.23 | async-start | bytes 2359296 | tf_op jit(solution)/shard_map/all_gather | solution.py:105
  58.0 58.2 %copy-start.2 = (bf16[2,256,2048]{2,1,0:T(8,128)(2,1)S(1)}, bf16[2,256,2048]{2,1,0:T(8,128)(2,1)}, u32[]{:S(2)}) copy-start(bf16[2,256,2048]{2,1,0:T(8,128)(2,1)} %all-gather.12.cloned.1.call-done) | copy-start | bytes 6291460
  90.0 42.8 %copy-start.9 = (f32[2,256,512]{2,1,0:T(8,128)}, f32[2,256,512]{2,1,0:T(8,128)S(1)}, u32[]{:S(2)}) copy-start(f32[2,256,512]{2,1,0:T(8,128)S(1)} %get-tuple-element.91) | copy-start | bytes 3145732
  135.3 3.9 copy-start.11
  141.9 1.3 copy-start.26
  141.9 1.6 copy-start.27
  141.9 1.6 copy-start.28
  146.0 10.0 all-to-all-start.2
  156.0 10.1 all-to-all-start.1
  162.3 22.9 %copy-start.38 = (s32[2,1024]{1,0:T(2,128)S(1)}, s32[2,1024]{1,0:T(2,128)}, u32[]{:S(2)}) copy-start(s32[2,1024]{1,0:T(2,128)} %param.16) | copy-start | bytes 24580
  166.1 5.8 copy-start.31
  166.1 15.7 %all-to-all-start = ((bf16[2,256,4,128]{3,1,0,2:T(8,128)(2,1)}), bf16[2,256,4,128]{3,1,0,2:T(8,128)(2,1)}, u32[]{:S(2)}, u32[]{:S(2)}) async-start(bf16[2,256,4,128]{3,1,0,2:T(8,128)(2,1)} %bitcast.218), calls=%async_computation | async-start | bytes 1048576 | tf_op jit(solution)/shard_map/all_to_all | solution.py:143
  170.2 120.1 %reduce-scatter.12.cloned.1.call-start = ((), (), s32[]{:S(2)}) async-start(), calls=%async_computation.24 | async-start | bytes 5242880 | tf_op jit(solution)/shard_map/reduce_scatter | solution.py:79
  171.9 17.4 %copy-start.16 = (bf16[2,4,256,1,128]{4,2,1,0,3:T(8,128)(2,1)}, bf16[2,4,256,1,128]{4,2,1,0,3:T(8,128)(2,1)S(1)}, u32[]{:S(2)}) copy-start(bf16[2,4,256,1,128]{4,2,1,0,3:T(8,128)(2,1)S(1)} %copy.93) | copy-start | bytes 1572868
  185.3 5.2 copy-start.19
  189.3 3.3 copy-start
  194.1 19.8 %copy-start.14 = (bf16[2,128,1024]{2,1,0:T(8,128)(2,1)}, bf16[2,128,1024]{2,1,0:T(8,128)(2,1)S(1)}, u32[]{:S(2)}) copy-start(bf16[2,128,1024]{2,1,0:T(8,128)(2,1)S(1)} %convolution_convert_fusion.1) | copy-start | bytes 1572868
  213.9 77.8 %copy-start.18 = (bf16[2,64,2048]{2,1,0:T(8,128)(2,1)S(1)}, bf16[2,64,2048]{2,1,0:T(8,128)(2,1)}, u32[]{:S(2)}) copy-start(bf16[2,64,2048]{2,1,0:T(8,128)(2,1)} %param.15) | copy-start | bytes 1572868
  213.9 77.8 %copy-start.35 = (f32[2048]{0:T(1024)S(1)}, f32[2048]{0:T(1024)}, u32[]{:S(2)}) copy-start(f32[2048]{0:T(1024)} %param.27) | copy-start | bytes 24580
  214.0 133.1 %all-gather.24.cloned.1.call-start = ((), (), s32[]{:S(2)}) async-start(), calls=%async_computation.26 | async-start | bytes 9437184 | tf_op jit(solution)/shard_map/all_gather | solution.py:106
  214.7 180.1 %all-gather.22.cloned.1.call-start = ((), (), s32[]{:S(2)}) async-start(), calls=%async_computation.25 | async-start | bytes 2621440 | tf_op jit(solution)/shard_map/all_gather | solution.py:75
  294.0 155.8 %all-gather.26.cloned.1.call-start = ((), (), s32[]{:S(2)}) async-start(), calls=%async_computation.27 | async-start | bytes 9437184 | tf_op jit(solution)/shard_map/all_gather | solution.py:107
  294.7 211.1 %all-gather.28.cloned.1.call-start = ((), (), s32[]{:S(2)}) async-start(), calls=%async_computation.28 | async-start | bytes 9437184 | tf_op jit(solution)/shard_map/all_gather | solution.py:108
  295.3 298.0 %reduce-scatter.14.cloned.1.call-start = ((), (), s32[]{:S(2)}) async-start(), calls=%async_computation.29 | async-start | bytes 5242880 | tf_op jit(solution)/shard_map/reduce_scatter | solution.py:79
  516.4 78.4 %copy-start.4 = (bf16[2,64,2048]{2,1,0:T(8,128)(2,1)S(1)}, bf16[2,64,2048]{2,1,0:T(8,128)(2,1)}, u32[]{:S(2)}) copy-start(bf16[2,64,2048]{2,1,0:T(8,128)(2,1)} %param.29) | copy-start | bytes 1572868
  516.4 78.4 %copy-start.36 = (f32[2048]{0:T(1024)S(1)}, f32[2048]{0:T(1024)}, u32[]{:S(2)}) copy-start(f32[2048]{0:T(1024)} %param.28) | copy-start | bytes 24580
  516.4 128.6 %all-gather.30.cloned.1.call-start = ((), (), s32[]{:S(2)}) async-start(), calls=%async_computation.30 | async-start | bytes 2621440 | tf_op jit(solution)/shard_map/all_gather | solution.py:75
  598.7 152.0 %reduce-scatter.16.cloned.1.call-start = ((), (), s32[]{:S(2)}) async-start(), calls=%async_computation.31 | async-start | bytes 5242880 | tf_op jit(solution)/shard_map/reduce_scatter | solution.py:79
  656.9 8.5 copy-start.39
  656.9 8.5 copy-start.40
  674.9 77.8 %copy-start.3 = (f32[2,64,2048]{2,1,0:T(8,128)S(1)}, f32[2,64,2048]{2,1,0:T(8,128)}, u32[]{:S(2)}) copy-start(f32[2,64,2048]{2,1,0:T(8,128)} %reduce-scatter.14.cloned.1.call-done) | copy-start | bytes 3145732
  675.0 127.5 %all-gather.32.cloned.1.call-start = ((), (), s32[]{:S(2)}) async-start(), calls=%async_computation.32 | async-start | bytes 2621440 | tf_op jit(solution)/shard_map/all_gather | solution.py:75
  756.1 241.7 %reduce-scatter.24.cloned.1.call-start = ((), (), s32[]{:S(2)}) async-start(), calls=%async_computation.36 | async-start | bytes 4718592 | tf_op jit(solution)/shard_map/reduce_scatter | solution.py:296
  841.3 1.2 copy-start.15
  843.8 8.0 copy-start.17
  849.9 2.0 copy-start.1
  851.9 6.0 copy-start.29
  853.8 13.1 all-to-all-start.5
  866.9 14.5 all-to-all-start.6
  871.0 128.8 %reduce-scatter.22.cloned.1.call-start = ((), (), s32[]{:S(2)}) async-start(), calls=%async_computation.35 | async-start | bytes 4718592 | tf_op jit(solution)/shard_map/reduce_scatter | solution.py:295
  882.7 1.8 copy-start.12
  882.7 2.8 copy-start.10
  884.5 1.0 copy-start.6
  884.5 1.5 copy-start.7
  884.5 1.7 copy-start.8
  902.8 102.9 %reduce-scatter.20.cloned.1.call-start = ((), (), s32[]{:S(2)}) async-start(), calls=%async_computation.34 | async-start | bytes 4718592 | tf_op jit(solution)/shard_map/reduce_scatter | solution.py:294
  905.7 3.8 copy-start.21
  909.0 3.7 copy-start.23
  909.0 175.7 %reduce-scatter.18.cloned.1.call-start = ((), (), s32[]{:S(2)}) async-start(), calls=%async_computation.33 | async-start | bytes 5242880 | tf_op jit(solution)/shard_map/reduce_scatter | solution.py:79
  909.5 3.2 copy-start.30
  912.7 1.3 copy-start.25
  912.7 1.9 copy-start.34
  918.0 1.0 copy-start.33
  918.0 222.3 %reduce-scatter.26.cloned.1.call-start = ((), (), s32[]{:S(2)}) async-start(), calls=%async_computation.37 | async-start | bytes 4718592 | tf_op jit(solution)/shard_map/reduce_scatter | solution.py:297
  923.9 336.7 %reduce-scatter.32.cloned.1.call-start = ((), (), s32[]{:S(2)}) async-start(), calls=%async_computation.40 | async-start | bytes 18874368 | tf_op jit(solution)/shard_map/reduce_scatter | solution.py:300
  936.5 1.6 copy-start.37
  936.5 444.4 %reduce-scatter.28.cloned.1.call-start = ((), (), s32[]{:S(2)}) async-start(), calls=%async_computation.38 | async-start | bytes 18874368 | tf_op jit(solution)/shard_map/reduce_scatter | solution.py:298
  948.0 553.3 %reduce-scatter.30.cloned.1.call-start = ((), (), s32[]{:S(2)}) async-start(), calls=%async_computation.39 | async-start | bytes 18874368 | tf_op jit(solution)/shard_map/reduce_scatter | solution.py:299
  958.0 126.7 %copy-start.5 = (bf16[2,64,2048]{2,1,0:T(8,128)(2,1)S(1)}, bf16[2,64,2048]{2,1,0:T(8,128)(2,1)}, u32[]{:S(2)}) copy-start(bf16[2,64,2048]{2,1,0:T(8,128)(2,1)} %param.29) | copy-start | bytes 1572868
  958.0 126.7 %copy-start.13 = (f32[2,64,2048]{2,1,0:T(8,128)S(1)}, f32[2,64,2048]{2,1,0:T(8,128)}, u32[]{:S(2)}) copy-start(f32[2,64,2048]{2,1,0:T(8,128)} %reduce-scatter.16.cloned.1.call-done) | copy-start | bytes 3145732
  (4 other events, 3.2 us)
Sparse Core Ops, SparseCore 0:
  9.6 48.3 all-gather.11
  59.9 26.5 all-gather.15
  88.4 27.7 all-gather.17
  117.9 27.7 all-gather.13
  147.4 35.7 all-gather.19
  214.1 76.1 reduce-scatter.11
  292.2 54.7 all-gather.23
  349.1 45.6 all-gather.21
  396.7 53.0 all-gather.25
  451.6 54.2 all-gather.27
  516.5 76.7 reduce-scatter.13
  598.8 46.1 all-gather.29
  675.1 75.5 reduce-scatter.15
  756.2 46.1 all-gather.31
  841.4 54.3 reduce-scatter.23
  902.9 48.2 reduce-scatter.21
  954.5 51.2 reduce-scatter.19
  1007.9 76.7 reduce-scatter.17
  1088.6 51.6 reduce-scatter.25
  1144.3 116.1 reduce-scatter.31
  1264.7 116.1 reduce-scatter.27
  1385.1 116.1 reduce-scatter.29
where the time goes:
time: 1520 us; the launch traced here: 1510 us
  waiting for transfers between devices  1130 us (74%)
  matrix products  159 us (10%)
  blocking collectives  93.2 us (6%)
  local copies, waits for them, and re-layouts  49.8 us (3%)
  other arithmetic  35.7 us (2%)
  starting transfers between devices  21.8 us (1%)
    reduce_scatter x4, waiting for transfers between devices, sum_tokens(): return lax.psum_scatter(terms, 'tensor', scatter_dimension=1, tiled=True)  305 us
    all_gather x4, waiting for transfers between devices, gather_tokens(): return lax.all_gather(matrix_rows, 'tensor', axis=1, tiled=True)  184 us
    reduce_scatter x1, waiting for transfers between devices, body(): lax.psum_scatter(gate_wgrad, ('fsdp', 'ctx'), scatter_dimension=0, tiled=...  120 us
    reduce_scatter x1, waiting for transfers between devices, body(): lax.psum_scatter(up_wgrad, ('fsdp', 'ctx'), scatter_dimension=0, tiled=True)  120 us
    reduce_scatter x1, waiting for transfers between devices, body(): lax.psum_scatter(down_wgrad, ('fsdp', 'ctx'), scatter_dimension=0, tiled=...  120 us
    reduce_scatter x1, waiting for transfers between devices, body(): lax.psum_scatter(output_wgrad, ('fsdp', 'ctx'), scatter_dimension=0, tile...  53.2 us
    all_gather x1, waiting for transfers between devices, body(): lax.all_gather(gate_weight, ('fsdp', 'ctx'), axis=0, tiled=True)  51.1 us
    dot_general x7, matrix products, project(): jnp.einsum('xmj,je->xme', matrix_rows, weight_matrix, preferred_element_t...  48.6 us
  transfers between devices with their start and end apart: 27, of which 23 were waited for; matrix products, arithmetic and copies ran while one was open for 11% of the time, Pallas kernels for 0%

commit v1 on v0

v1 whole, which is shorter than its diff:
```python
import functools

import jax
import jax.numpy as jnp
from jax import lax
from jax.experimental import pallas as pl
from jax.experimental.pallas import tpu as pltpu
from jax.sharding import PartitionSpec as P

D = 2048
HD = 128


epsilon = 1e-06
rope_theta = 500000.0
masked_score = -1e30


def rope_tables(position_ids):
    freq_index = jnp.arange(HD // 2, dtype=jnp.float32)
    inverse = rope_theta ** (-2.0 * freq_index / HD)
    angles = position_ids.astype(jnp.float32)[..., None] * inverse
    return (jnp.cos(angles), jnp.sin(angles))


MESH = pl.DeviceIdType.MESH
BF = jnp.bfloat16
F32 = jnp.float32
VMEM_SPEC = pl.BlockSpec(memory_space=pltpu.VMEM)
HBM_SPEC = pl.BlockSpec(memory_space=pltpu.HBM)
NN = (((1,), (0,)), ((), ()))
NT = (((1,), (1,)), ((), ()))
TN = (((0,), (0,)), ((), ()))


def dot(a, b, dims):
    return lax.dot_general(a, b, dims, preferred_element_type=F32)


def loop(count, step):
    def run(i, carry):
        step(i)
        return carry

    lax.fori_loop(0, count, run, 0)


def cut(i, size):
    return pl.ds(pl.multiple_of(i * size, size), size)


def both(*conds):
    out = True
    for cond in conds:
        if isinstance(cond, bool):
            if not cond:
                return False
        elif isinstance(out, bool):
            out = cond
        else:
            out = jnp.logical_and(out, cond)
    return out


def when(cond, step):
    if isinstance(cond, bool):
        if cond:
            step()
    else:
        pl.when(cond)(step)


class Place:
    def __init__(self, fsdp_size, ctx_size, tensor_size):
        self.nf, self.nc, self.nt = fsdp_size, ctx_size, tensor_size
        self.f = lax.axis_index("fsdp")
        self.c = lax.axis_index("ctx")
        self.t = lax.axis_index("tensor")
        self.p = lax.rem(self.f, 2)
        self.group = self.f - self.p
        self.mate = self.group + 1 - self.p

    def at(self, f=None, c=None, t=None):
        return {
            "fsdp": self.f if f is None else f,
            "ctx": self.c if c is None else c,
            "tensor": self.t if t is None else t,
        }

    def plane(self):
        out = []
        for dg in range(self.nf // 2):
            for dc in (3, 1, 2, 0) if self.nc == 4 else range(self.nc):
                for dp in (0, 1):
                    if dg or dc or dp:
                        out.append((dg, dc, dp))
        return out

    def peer(self, off):
        dg, dc, dp = off
        group = lax.rem(self.group + 2 * dg, self.nf)
        core = self.p + dp - 2 * self.p * dp
        return group + core, core, jnp.bitwise_xor(self.c, dc)

    def barrier(self):
        sem = pltpu.get_barrier_semaphore()

        def signal(**place):
            pl.semaphore_signal(sem, inc=1, device_id=self.at(**place), device_id_type=MESH)

        offs = self.plane()
        for off in offs:
            f, _, c = self.peer(off)
            signal(f=f, c=c)
        for dt in range(1, self.nt):
            for core in range(2):
                signal(f=self.group + core, t=lax.rem(self.t + dt, self.nt))
        pl.semaphore_wait(sem, len(offs) + 2 * (self.nt - 1))


def remote(src, dst, send, recv, device):
    return pltpu.make_async_remote_copy(
        src_ref=src, dst_ref=dst, send_sem=send, recv_sem=recv, device_id=device, device_id_type=MESH
    )


def wait_bytes(ref, sem):
    pltpu.make_async_copy(ref, ref, sem).wait()


class Reduce:
    def __init__(self, e, part, pair, right, left, sems, rows):
        self.e, self.part, self.pair, self.right, self.left, self.rows = e, part, pair, right, left, rows
        self.sems = sems

    def half(self, p):
        n = self.e.nt * self.rows
        return self.part.at[pl.ds(pl.multiple_of(p * n, n), n), :]

    def block(self, b):
        return self.part.at[cut(self.e.p * self.e.nt + b, self.rows), :]

    def _pair(self):
        return remote(
            self.half(1 - self.e.p), self.pair, self.sems.at[0, 0], self.sems.at[1, 0],
            self.e.at(f=self.e.mate),
        )

    def _side(self, b, k, up):
        e = self.e
        buf, row = (self.right, 0) if up else (self.left, 2)
        return remote(
            self.block(b), buf.at[k], self.sems.at[row, 1 + k], self.sems.at[row + 1, 1 + k],
            e.at(t=e.t + 1 if up else e.t - 1),
        )

    def pair_send(self):
        self._pair().start()

    def pair_add(self):
        self._pair().wait_recv()
        mine = self.half(self.e.p)

        def step(i):
            sl = cut(i, self.rows)
            mine[sl, :] = (mine[sl, :].astype(F32) + self.pair[sl, :].astype(F32)).astype(BF)

        loop(self.e.nt, step)

    def slot(self, j):
        e, n = self.e, self.e.nt
        for up in (True, False):
            b = e.t + (n - 2) - j if up else e.t - (n - 2) + j
            near = e.t > 0 if up else e.t < n - 1
            far = e.t < n - 1 if up else e.t > 0
            inside = b <= n - 1 if up else b >= 0
            buf = self.right if up else self.left

            def take(b=b, buf=buf, up=up):
                self._side(b, j, up).wait_recv()

                def add():
                    blk = self.block(b)
                    blk[...] = (blk[...].astype(F32) + buf[j].astype(F32)).astype(BF)

                when(j < n - 2, add)

            when(both(j >= 0, j <= n - 2, near, inside), take)
            when(both(j < n - 2, far, inside), lambda b=b, up=up: self._side(b, j + 1, up).start())

    def result(self, out):
        e, n = self.e, self.e.nt
        out[...] = self.block(e.t)[...].astype(F32)

        def add_right():
            out[...] += self.right[n - 2].astype(F32)

        def add_left():
            out[...] += self.left[n - 2].astype(F32)

        when(e.t > 0, add_right)
        when(e.t < n - 1, add_left)

    def drain(self):
        e, n = self.e, self.e.nt
        self._pair().wait_send()

        def step(i):
            j = i - 1
            for up in (True, False):
                b = e.t + (n - 2) - j if up else e.t - (n - 2) + j
                far = e.t < n - 1 if up else e.t > 0
                inside = b <= n - 1 if up else b >= 0
                when(both(far, inside), lambda b=b, up=up: self._side(b, j + 1, up).wait_send())

        for i in range(n - 1):
            step(i)


class Gather:
    def __init__(self, e, full, sems, rows):
        self.e, self.full, self.sems, self.rows = e, full, sems, rows

    def block(self, p, b):
        return self.full.at[cut(p * self.e.nt + b, self.rows), :]

    def _side(self, b, k, up):
        e = self.e
        row = 0 if up else 2
        ref = self.block(e.p, b)
        return remote(
            ref, ref, self.sems.at[row, k], self.sems.at[row + 1, k],
            e.at(t=e.t + 1 if up else e.t - 1),
        )

    def _pair(self, b, k, incoming):
        e = self.e
        ref = self.block(1 - e.p if incoming else e.p, b)
        return remote(ref, ref, self.sems.at[4, k], self.sems.at[5, k], e.at(f=e.mate))

    def init(self):
        e, n = self.e, self.e.nt
        when(e.t < n - 1, lambda: self._side(e.t, 0, True).start())
        when(e.t > 0, lambda: self._side(e.t, 0, False).start())
        self._pair(e.t, 0, False).start()

    def slot(self, j):
        e, n = self.e, self.e.nt
        for up in (True, False):
            b = e.t - 1 - j if up else e.t + 1 + j
            inside = b >= 0 if up else b <= n - 1
            far = e.t < n - 1 if up else e.t > 0
            k = 1 + j if up else n + j

            def take(b=b, up=up, far=far, k=k):
                self._side(b, j, up).wait_recv()
                when(both(far, j < n - 2), lambda: self._side(b, j + 1, up).start())
                self._pair(b, k, False).start()

            when(both(j >= 0, j <= n - 2, inside), take)

    def _rest(self, step_pair):
        e, n = self.e, self.e.nt
        step_pair(e.t, 0)
        for j in range(n - 1):
            when(e.t - 1 - j >= 0, lambda j=j: step_pair(e.t - 1 - j, 1 + j))
            when(e.t + 1 + j <= n - 1, lambda j=j: step_pair(e.t + 1 + j, n + j))

    def done(self):
        self._rest(lambda b, k: self._pair(b, k, True).wait_recv())

    def drain(self):
        e, n = self.e, self.e.nt
        self._rest(lambda b, k: self._pair(b, k, False).wait_send())
        when(e.t < n - 1, lambda: self._side(e.t, 0, True).wait_send())
        when(e.t > 0, lambda: self._side(e.t, 0, False).wait_send())
        for j in range(n - 2):
            when(
                both(e.t - 1 - j >= 0, e.t < n - 1),
                lambda j=j: self._side(e.t - 1 - j, j + 1, True).wait_send(),
            )
            when(
                both(e.t + 1 + j <= n - 1, e.t > 0),
                lambda j=j: self._side(e.t + 1 + j, j + 1, False).wait_send(),
            )


class Weight:
    def __init__(self, e, shard, full, send, recv):
        self.e, self.shard, self.full, self.send, self.recv = e, shard, full, send, recv
        self.rows, self.half = shard.shape[0], full.shape[1]

    def start(self):
        e = self.e
        dst = self.full.at[cut(e.f * e.nc + e.c, self.rows), :]
        for off in e.plane():
            f, core, c = e.peer(off)
            remote(
                self.shard.at[:, cut(core, self.half)], dst, self.send, self.recv, e.at(f=f, c=c)
            ).start()
        pltpu.make_async_copy(self.shard.at[:, cut(e.p, self.half)], dst, self.recv).start()

    def wait(self):
        wait_bytes(self.full, self.recv)

    def drain(self):
        count = len(self.e.plane()) * self.rows
        wait_bytes(self.full.at[pl.ds(0, count), :], self.send)


def ffn_kernel(
    sizes, seqs, rows,
    att, wo_sh, gate_sh, up_sh, down_sh, tokens, cot, again, fgain,
    block_out, hidden_grad, agh, wo_part, gate_part, up_part, down_part, gains,
    wo_v, g_v, u_v, d_v, part, pair, right, left, hid, mgr, agr, aa, bb, mixed,
    unit1, hid32, scale1, scratch_y, agx,
    wsem, rsem, gsem, xsend, xrecv, osem,
):
    e = Place(*sizes)
    dm = tokens.shape[2]
    half = g_v.shape[1]
    wide = att.shape[2]
    heads = wide // HD
    weights = [
        Weight(e, sh, full, wsem.at[i, 0], wsem.at[i, 1])
        for i, (sh, full) in enumerate(
            ((wo_sh, wo_v), (gate_sh, g_v), (up_sh, u_v), (down_sh, d_v))
        )
    ]
    w_o, w_g, w_u, w_d = weights

    def reduce(k, s):
        return Reduce(e, part.at[s], pair.at[s], right.at[s], left.at[s], rsem.at[k, s], rows)

    def gather(k, s):
        return Gather(e, (hid, mgr, agr)[k].at[s], gsem.at[k, s], rows)

    red = [[reduce(k, s) for s in range(seqs)] for k in range(3)]
    gat = [[gather(k, s) for s in range(seqs)] for k in range(3)]

    e.barrier()
    for w in weights:
        w.start()
    gains[...] = jnp.zeros_like(gains)

    tile = 512

    def out_tiles(s):
        def step(i):
            sl = cut(i, tile)
            part[s, :, sl] = dot(att[s], wo_v[sl, :], NT).astype(BF)

        loop(dm // tile, step)

    def norm1(s):
        y = scratch_y
        red[0][s].result(y)
        v = y[...]
        scale = lax.rsqrt(jnp.mean(v * v, axis=-1, keepdims=True) + epsilon)
        unit = v * scale
        unit1[s] = unit
        scale1[s] = jnp.broadcast_to(scale, scale1.shape[1:])
        h = tokens[s].astype(F32) + unit * again[...]
        hid32[s] = h
        gat[0][s].block(e.p, e.t)[...] = h.astype(BF)

    def ffn_tile(s, i):
        sl = cut(i, 256)
        gate = dot(hid[s], g_v[:, sl], NN)
        up = dot(hid[s], u_v[:, sl], NN)
        sig = jax.nn.sigmoid(gate)
        act = gate * sig
        mixed[s, :, sl] = (act * up).astype(BF)
        aa[s, :, sl] = (up * sig * (1.0 + gate * (1.0 - sig))).astype(BF)
        bb[s, :, sl] = act.astype(BF)

    ffn_tiles = half // 256

    def down_tiles(s):
        def step(i):
            sl = cut(i, tile)
            part[s, :, sl] = dot(mixed[s], d_v[sl, :], NT).astype(BF)

        loop(dm // tile, step)

    def norm2(s):
        y = scratch_y
        red[1][s].result(y)
        v = y[...]
        scale = lax.rsqrt(jnp.mean(v * v, axis=-1, keepdims=True) + epsilon)
        unit = v * scale
        block_out[s] = (hid32[s] + unit * fgain[...]).astype(BF)
        upstream = cot[s].astype(F32)
        gains[3:4, :] += jnp.sum(upstream * unit, axis=0, keepdims=True)
        g = upstream * fgain[...]
        m = scale * (g - unit * jnp.mean(g * unit, axis=-1, keepdims=True))
        gat[1][s].block(e.p, e.t)[...] = m.astype(BF)

    def inner_tiles(s):
        def step(i):
            sl = cut(i, 256)
            inner = dot(mgr[s], d_v[:, sl], NN)
            aa[s, :, sl] = (inner * aa[s, :, sl].astype(F32)).astype(BF)
            bb[s, :, sl] = (inner * bb[s, :, sl].astype(F32)).astype(BF)

        loop(ffn_tiles, step)

    def back_tiles(s):
        def step(i):
            sl = cut(i, tile)
            part[s, :, sl] = (dot(aa[s], g_v[sl, :], NT) + dot(bb[s], u_v[sl, :], NT)).astype(BF)

        loop(dm // tile, step)

    def norm3(s):
        y = scratch_y
        red[2][s].result(y)
        hg = cot[s].astype(F32) + y[...]
        hidden_grad[s] = hg
        unit = unit1[s]
        gains[2:3, :] += jnp.sum(hg * unit, axis=0, keepdims=True)
        g = hg * again[...]
        scale = scale1[s][:, 0:1]
        a = scale * (g - unit * jnp.mean(g * unit, axis=-1, keepdims=True))
        gat[2][s].block(e.p, e.t)[...] = a.astype(BF)

    def weight_tile(left_rows, right_rows, out, i, width):
        per = out.shape[1] // width
        sl, cl = cut(lax.div(i, per), tile), cut(lax.rem(i, per), width)
        lhs = left_rows[:, :, sl].reshape(-1, tile)
        rhs = right_rows[:, :, cl].reshape(-1, width)
        out[sl, cl] = dot(lhs, rhs, TN).astype(BF)

    n = e.nt
    span = agh.shape[2]

    def heads_copy(s, jj, q):
        src = agx.at[s, jj, pl.ds(q * span, span), :]
        dst = agh.at[s, e.c]
        return src, dst

    def heads_grad(s):
        r = dot(agr[s], wo_v[...], NN).astype(BF)
        for jj in range(heads):
            agx[s, jj] = r[:, jj * HD : (jj + 1) * HD]
        for jj in range(heads):
            head = heads * e.p + jj
            for q in range(2):
                src, dst = heads_copy(s, jj, q)
                self_here = both(head == e.c, q == e.p)

                def local(src=src, dst=dst):
                    pltpu.make_async_copy(src, dst, xrecv.at[s]).start()

                def away(src=src, dst=dst, q=q, head=head, jj=jj):
                    remote(
                        src, dst, xsend.at[s, jj, q], xrecv.at[s], e.at(f=e.group + q, c=head)
                    ).start()

                when(self_here, local)
                when(jnp.logical_not(self_here), away)

    def heads_wait(s):
        wait_bytes(agh.at[s], xrecv.at[s])
        block = agx.at[s, 0, pl.ds(0, span), :]
        for jj in range(heads):
            head = heads * e.p + jj
            for q in range(2):
                when(
                    jnp.logical_not(both(head == e.c, q == e.p)),
                    lambda jj=jj, q=q: wait_bytes(block, xsend.at[s, jj, q]),
                )

    w_o.wait()
    out_tiles(0)
    red[0][0].pair_send()
    out_tiles(1)
    red[0][0].pair_add()
    red[0][1].pair_send()

    def step(i):
        red[0][0].slot(i - 1)

    loop(n, step)
    red[0][1].pair_add()
    norm1(0)
    gat[0][0].init()

    def step(i):
        red[0][1].slot(i - 1)
        gat[0][0].slot(i - 1)

    loop(n, step)
    gat[0][0].done()
    norm1(1)
    gat[0][1].init()
    w_g.wait()
    w_u.wait()

    def step(i):
        ffn_tile(0, i)
        gat[0][1].slot(i)

    loop(ffn_tiles, step)
    w_d.wait()
    red[0][0].drain()
    down_tiles(0)
    red[1][0].pair_send()
    gat[0][1].done()
    ffn_tile(1, 0)
    red[1][0].pair_add()

    def step(i):
        red[1][0].slot(i - 1)
        ffn_tile(1, i + 1)

    loop(ffn_tiles - 1, step)
    for j in range(ffn_tiles - 2, n - 1):
        red[1][0].slot(j)
    norm2(0)
    gat[1][0].init()
    red[0][1].drain()
    down_tiles(1)
    red[1][1].pair_send()
    gat[1][0].slot(0)
    red[1][1].pair_add()

    def step(i):
        red[1][1].slot(i - 1)
        gat[1][0].slot(i + 1)

    loop(n, step)
    norm2(1)
    gat[1][1].init()
    gat[1][0].done()
    inner_tiles(0)
    red[1][0].drain()
    back_tiles(0)
    red[2][0].pair_send()
    gat[1][1].slot(0)
    red[2][0].pair_add()

    def step(i):
        red[2][0].slot(i - 1)
        gat[1][1].slot(i + 1)

    loop(n - 2, step)
    gat[1][1].done()
    inner_tiles(1)
    red[2][0].slot(n - 3)
    red[1][1].drain()
    back_tiles(1)
    red[2][1].pair_send()
    red[2][0].slot(n - 2)
    norm3(0)
    gat[2][0].init()
    red[2][1].pair_add()

    def step(i):
        red[2][1].slot(i - 1)
        gat[2][0].slot(i - 1)

        def fill(k):
            weight_tile(mgr, mixed, d_v, 2 * i + k, tile)
            weight_tile(hid, aa, g_v, 2 * i + k, tile)

        loop(2, fill)

    loop(n, step)
    out_d = pltpu.make_async_copy(d_v, down_part, osem.at[0])
    out_g = pltpu.make_async_copy(g_v, gate_part, osem.at[1])
    out_d.start()
    out_g.start()
    norm3(1)
    gat[2][1].init()
    gat[2][0].done()
    heads_grad(0)

    def step(i):
        gat[2][1].slot(i - 1)
        loop(2, lambda k: weight_tile(hid, bb, u_v, 2 * i + k, tile))

    loop(n, step)
    out_u = pltpu.make_async_copy(u_v, up_part, osem.at[2])
    out_u.start()
    gat[2][1].done()
    heads_grad(1)
    loop(dm // tile, lambda i: weight_tile(agr, att, wo_v, i, wide))
    out_o = pltpu.make_async_copy(wo_v, wo_part, osem.at[3])
    out_o.start()
    heads_wait(0)
    heads_wait(1)
    red[2][0].drain()
    red[2][1].drain()
    for k in range(3):
        for s in range(seqs):
            gat[k][s].drain()
    for w in weights:
        w.drain()
    for o in (out_d, out_g, out_u, out_o):
        o.wait()


def ffn_stage(sizes, att, wo_sh, gate_sh, up_sh, down_sh, tokens, cot, again, fgain):
    nf, nc, nt = sizes
    seqs, rows, dm = tokens.shape
    half = gate_sh.shape[1] // 2
    wide = wo_sh.shape[1] // 2
    full = 2 * nt * rows
    sds = jax.ShapeDtypeStruct
    v, dma = pltpu.VMEM, pltpu.SemaphoreType.DMA
    return pl.pallas_call(
        functools.partial(ffn_kernel, sizes, seqs, rows),
        name="ffn_stage",
        out_shape=(
            sds((seqs, rows, dm), BF),
            sds((seqs, rows, dm), F32),
            sds((seqs, nc, nt * rows, HD), BF),
            sds((dm, wide), BF),
            sds((dm, half), BF),
            sds((dm, half), BF),
            sds((dm, half), BF),
            sds((8, dm), F32),
        ),
        in_specs=[VMEM_SPEC] + [HBM_SPEC] * 4 + [VMEM_SPEC] * 4,
        out_specs=(VMEM_SPEC, VMEM_SPEC) + (HBM_SPEC,) * 5 + (VMEM_SPEC,),
        scratch_shapes=[
            v((dm, wide), BF),
            v((dm, half), BF),
            v((dm, half), BF),
            v((dm, half), BF),
            v((seqs, full, dm), BF),
            v((seqs, nt * rows, dm), BF),
            v((seqs, nt - 1, rows, dm), BF),
            v((seqs, nt - 1, rows, dm), BF),
            v((seqs, full, dm), BF),
            v((seqs, full, dm), BF),
            v((seqs, full, dm), BF),
            v((seqs, full, half), BF),
            v((seqs, full, half), BF),
            v((seqs, full, half), BF),
            v((seqs, rows, dm), F32),
            v((seqs, rows, dm), F32),
            v((seqs, rows, 128), F32),
            v((rows, dm), F32),
            v((seqs, wide // HD, full, HD), BF),
            dma((4, 2)),
            dma((3, seqs, 4, nt)),
            dma((3, seqs, 6, 2 * nt - 1)),
            dma((seqs, wide // HD, 2)),
            dma((seqs,)),
            dma((4,)),
        ],
        compiler_params=pltpu.CompilerParams(
            collective_id=1, has_side_effects=True, vmem_limit_bytes=63 << 20
        ),
    )(att, wo_sh, gate_sh, up_sh, down_sh, tokens, cot, again, fgain)


class Exchange:
    def __init__(self, e, mine, inbox, send, recv, members, own):
        self.e, self.mine, self.inbox, self.send, self.recv = e, mine, inbox, send, recv
        self.members, self.own = members, own

    @staticmethod
    def plane(e):
        out = []
        for f in range(e.nf):
            for c in range(e.nc):
                out.append((f * e.nc + c, e.at(f=f, c=c), both(e.f == f, e.c == c)))
        return out, e.f * e.nc + e.c

    @staticmethod
    def heads(e):
        out = []
        for q in range(2):
            for t in range(e.nt):
                out.append((q * e.nt + t, e.at(f=e.group + q, t=t), both(e.p == q, e.t == t)))
        return out, e.p * e.nt + e.t

    @staticmethod
    def line(e):
        return [(t, e.at(t=t), e.t == t) for t in range(e.nt)], e.t

    def start(self):
        self.inbox[self.own] = self.mine[...]
        for k, device, me in self.members:

            def go(k=k, device=device):
                remote(
                    self.mine, self.inbox.at[self.own], self.send.at[k], self.recv.at[self.own], device
                ).start()

            when(jnp.logical_not(me), go)

    def finish(self):
        for k, device, me in self.members:

            def go(k=k, device=device):
                d = remote(self.mine, self.inbox.at[k], self.send.at[k], self.recv.at[k], device)
                d.wait_recv()
                d.wait_send()

            when(jnp.logical_not(me), go)
        return jnp.sum(self.inbox[...], axis=0)


def to_heads(e, src, dst, send, recv, heads, span):
    for jj in range(heads):
        head = heads * e.p + jj
        for q in range(2):
            piece = src.at[jj, pl.ds(q * span, span), :]
            here = both(head == e.c, q == e.p)
            when(here, lambda piece=piece: pltpu.make_async_copy(piece, dst.at[e.c], recv).start())

            def away(piece=piece, jj=jj, q=q, head=head):
                remote(
                    piece, dst.at[e.c], send.at[jj, q], recv, e.at(f=e.group + q, c=head)
                ).start()

            when(jnp.logical_not(here), away)


def to_heads_drain(e, src, send, heads, span):
    piece = src.at[0, pl.ds(0, span), :]
    for jj in range(heads):
        head = heads * e.p + jj
        for q in range(2):
            here = both(head == e.c, q == e.p)
            when(jnp.logical_not(here), lambda jj=jj, q=q: wait_bytes(piece, send.at[jj, q]))


def from_heads(e, src, dst, send, recv, heads):
    core = lax.div(e.c, heads)
    for c in range(e.nc):
        here = both(e.c == c, core == e.p)
        when(here, lambda c=c: pltpu.make_async_copy(src.at[c], dst, recv).start())

        def away(c=c):
            remote(src.at[c], dst, send.at[c], recv, e.at(f=e.group + core, c=c)).start()

        when(jnp.logical_not(here), away)


def from_heads_drain(e, src, send, heads):
    core = lax.div(e.c, heads)
    for c in range(e.nc):
        here = both(e.c == c, core == e.p)
        when(jnp.logical_not(here), lambda c=c: wait_bytes(src.at[c], send.at[c]))


def columns(first, second):
    lane = lax.broadcasted_iota(jnp.int32, (first.shape[0], 128), 1)
    both_cols = jnp.where(lane == 0, first, jnp.where(lane == 1, second, 0.0))
    return both_cols.T[0:8]


def turn(values, angle_cos, angle_sin):
    return values * angle_cos + pltpu.roll(values, HD // 2, 1) * angle_sin


def turn_back(values, angle_cos, angle_sin):
    return values * angle_cos - pltpu.roll(values, HD // 2, 1) * angle_sin


def masked(scores, seg_col, seg_row, s, i, span):
    keys = scores.shape[1]
    row = lax.broadcasted_iota(jnp.int32, scores.shape, 0) + i * span
    col = lax.broadcasted_iota(jnp.int32, scores.shape, 1)
    same = seg_col[s, pl.ds(i * span, span), :] == seg_row[s, :, pl.ds(0, keys)]
    return jnp.where(jnp.logical_and(same, row >= col), scores, masked_score)


def front_kernel(
    sizes, seqs, rows,
    tokens, cos_own, sin_own, qgain, kgain, seg_col, seg_row, wq_sh, wk_sh, wv_sh,
    att, xs_out, wq_out, wk_out, wv_out, units, scales, angles, qkv_heads, att_heads, lse,
    x, wq, wk, wv, lin, qkvx, qkvh, atth, mine, inbox, wide_t, ang,
    wsem, gsem, asem, esem, hsend, hrecv, bsend, brecv, osem,
):
    e = Place(*sizes)
    n = e.nt
    span = n * rows
    wide = wq.shape[1]
    heads = wide // HD
    ws = [
        Weight(e, sh, full, wsem.at[i, 0], wsem.at[i, 1])
        for i, (sh, full) in enumerate(((wq_sh, wq), (wk_sh, wk), (wv_sh, wv)))
    ]
    gat = [Gather(e, x.at[s], gsem.at[s], rows) for s in range(seqs)]
    own = pl.ds(pl.multiple_of(e.p * span, span), span)

    def angle_copy():
        ref = ang.at[:, :, own, :]
        return remote(ref, ref, asem.at[0], asem.at[1], e.at(f=e.mate))

    e.barrier()
    for s in range(seqs):
        gat[s].block(e.p, e.t)[...] = tokens[s]
        gat[s].init()
    for w in (ws[2], ws[0], ws[1]):
        w.start()
    ang[0, :, own, :] = cos_own[...]
    ang[1, :, own, :] = sin_own[...]
    angle_copy().start()
    wide_t[...] = jnp.zeros_like(wide_t)

    def step(j):
        for s in range(seqs):
            gat[s].slot(j)

    loop(n - 1, step)
    for s in range(seqs):
        gat[s].done()
    outs = [pltpu.make_async_copy(x, xs_out, osem.at[0])]
    outs[0].start()
    ws[2].wait()
    for s in range(seqs):
        r = dot(x[s], wv[...], NN).astype(BF)
        for jj in range(heads):
            qkvx[2, s, jj] = r[:, jj * HD : (jj + 1) * HD]
        to_heads(e, qkvx.at[2, s], qkvh.at[2, s], hsend.at[2, s], hrecv.at[2, s], heads, span)
    ws[0].wait()
    ws[1].wait()
    for k, (w, out) in enumerate(((wq, wq_out), (wk, wk_out), (wv, wv_out))):
        outs.append(pltpu.make_async_copy(w, out, osem.at[1 + k]))
        outs[-1].start()
    sums = [[], []]
    for k, w in enumerate((wq, wk)):
        for s in range(seqs):
            r = dot(x[s], w[...], NN)
            lin[k, s] = r
            sums[k].append(jnp.sum(r * r, axis=-1, keepdims=True))
    mine[...] = columns(*[jnp.concatenate(v, axis=0) for v in sums])
    ex = Exchange(e, mine, inbox, esem.at[0], esem.at[1], *Exchange.heads(e))
    ex.start()
    angle_copy().wait_recv()
    angles[...] = ang[...]
    wide_t[0:8] = lax.rsqrt(ex.finish() / D + epsilon)
    sc = wide_t[...].T
    for s in range(seqs):
        scales[s] = sc[s * 2 * span : (s + 1) * 2 * span]
    place = cut(e.t * 2 + e.p, wide)
    for s in range(seqs):
        for k, gain in enumerate((qgain, kgain)):
            unit = lin[k, s] * scales[s][:, k : k + 1]
            units[k, s] = unit
            scaled = unit * gain[:, place]
            for jj in range(heads):
                turned = turn(scaled[:, jj * HD : (jj + 1) * HD], ang[0, s], ang[1, s])
                qkvx[k, s, jj] = turned.astype(BF)
            to_heads(e, qkvx.at[k, s], qkvh.at[k, s], hsend.at[k, s], hrecv.at[k, s], heads, span)

    for s in range(seqs):
        for k in (2, 0, 1):
            wait_bytes(qkvh.at[k, s], hrecv.at[k, s])
        for i in range(e.nc):
            keys = (i + 1) * span
            kb = qkvh[1, s, 0 : i + 1].reshape(keys, HD)
            vb = qkvh[2, s, 0 : i + 1].reshape(keys, HD)
            scores = masked(dot(qkvh[0, s, i], kb, NT) * HD**-0.5, seg_col, seg_row, s, i, span)
            top = jnp.max(scores, axis=-1, keepdims=True)
            ex_s = jnp.exp(scores - top)
            total = jnp.sum(ex_s, axis=-1, keepdims=True)
            log_total = top + jnp.log(total)
            lse[s, i * span : (i + 1) * span, :] = jnp.broadcast_to(log_total, (span, HD))
            probs = (ex_s * (1.0 / total)).astype(BF)
            atth[s, i] = dot(probs, vb, NN).astype(BF)
        dst = att.at[s, own, cut(lax.rem(e.c, heads), HD)]
        from_heads(e, atth.at[s], dst, bsend.at[s], brecv.at[s], heads)
    for k, (a, b) in enumerate(((qkvh, qkv_heads), (atth, att_heads))):
        outs.append(pltpu.make_async_copy(a, b, osem.at[4 + k]))
        outs[-1].start()
    for s in range(seqs):
        wait_bytes(att.at[s], brecv.at[s])
        from_heads_drain(e, atth.at[s], bsend.at[s], heads)
        for k in range(3):
            to_heads_drain(e, qkvx.at[k, s], hsend.at[k, s], heads, span)
        gat[s].drain()
    angle_copy().wait_send()
    for w in ws:
        w.drain()
    for o in outs:
        o.wait()


def front_stage(sizes, tokens, cos_own, sin_own, qgain, kgain, seg_col, seg_row, wq, wk, wv):
    nf, nc, nt = sizes
    seqs, rows, dm = tokens.shape
    wide = wq.shape[1] // 2
    heads = wide // HD
    full = 2 * nt * rows
    span = nt * rows
    sds = jax.ShapeDtypeStruct
    v, dma = pltpu.VMEM, pltpu.SemaphoreType.DMA
    return pl.pallas_call(
        functools.partial(front_kernel, sizes, seqs, rows),
        name="front_stage",
        out_shape=(
            sds((seqs, full, wide), BF),
            sds((seqs, full, dm), BF),
            sds((dm, wide), BF),
            sds((dm, wide), BF),
            sds((dm, wide), BF),
            sds((2, seqs, full, wide), F32),
            sds((seqs, full, 128), F32),
            sds((2, seqs, full, HD), F32),
            sds((3, seqs, nc, span, HD), BF),
            sds((seqs, nc, span, HD), BF),
            sds((seqs, nc * span, HD), F32),
        ),
        in_specs=[VMEM_SPEC] * 7 + [HBM_SPEC] * 3,
        out_specs=(HBM_SPEC,) * 5 + (VMEM_SPEC,) * 3 + (HBM_SPEC,) * 2 + (VMEM_SPEC,),
        scratch_shapes=[
            v((seqs, full, dm), BF),
            v((dm, wide), BF),
            v((dm, wide), BF),
            v((dm, wide), BF),
            v((2, seqs, full, wide), F32),
            v((3, seqs, heads, full, HD), BF),
            v((3, seqs, nc, span, HD), BF),
            v((seqs, nc, span, HD), BF),
            v((8, seqs * full), F32),
            v((2 * nt, 8, seqs * full), F32),
            v((128, seqs * full), F32),
            v((2, seqs, full, HD), F32),
            dma((3, 2)),
            dma((seqs, 6, 2 * nt - 1)),
            dma((2,)),
            dma((2, 2 * nt)),
            dma((3, seqs, heads, 2)),
            dma((3, seqs)),
            dma((seqs, nc)),
            dma((seqs,)),
            dma((6,)),
        ],
        compiler_params=pltpu.CompilerParams(
            collective_id=2, has_side_effects=True, vmem_limit_bytes=60 << 20
        ),
    )(tokens, cos_own, sin_own, qgain, kgain, seg_col, seg_row, wq, wk, wv)


class Scatter:
    def __init__(self, e, part, inbox, send, recv):
        self.e, self.part, self.inbox, self.send, self.recv = e, part, inbox, send, recv
        self.rows, self.half = inbox.shape[1], part.shape[1]

    def piece(self, f, c):
        return self.part.at[cut(f * self.e.nc + c, self.rows), :]

    def start(self):
        e = self.e
        slot = lax.div(e.group, 2) * e.nc + e.c
        dst = self.inbox.at[slot, :, cut(e.p, self.half)]
        for off in e.plane():
            f, _, c = e.peer(off)
            remote(self.piece(f, c), dst, self.send, self.recv, e.at(f=f, c=c)).start()
        pltpu.make_async_copy(self.piece(e.f, e.c), dst, self.recv).start()

    def wait(self):
        wait_bytes(self.inbox, self.recv)

    def drain(self):
        count = len(self.e.plane()) * self.rows
        wait_bytes(self.part.at[pl.ds(0, count), :], self.send)


def tail_kernel(
    sizes, seqs, rows,
    hidden_grad, gains_in, units, scales, angles, qgain, kgain, seg_col, seg_row, lse,
    agh_in, qkv_heads, att_heads, xs_in, wq_in, wk_in, wv_in,
    wo_part, gate_part, up_part, down_part,
    input_grad, gains_out, o_q, o_k, o_v, o_o, o_g, o_u, o_d,
    agh, qkvh, atth, x, wq, wk, wv, dh, dx, acck, accv, uu, pre, part, pair, right, left, y,
    mine, inbox, wide_t, gmine, gin, gin2, in_q, in_k, in_v, in_o, in_g, in_u, in_d, fin,
    lsem, dsend, drecv, esem, rsem, ssem, g1sem, g2sem, fsem,
):
    e = Place(*sizes)
    n = e.nt
    span = n * rows
    dm = x.shape[2]
    wide = wq.shape[1]
    heads = wide // HD
    scat = [
        Scatter(e, p, b, ssem.at[k, 0], ssem.at[k, 1])
        for k, (p, b) in enumerate(
            (
                (wq, in_q), (wk, in_k), (wv, in_v), (wo_part, in_o),
                (gate_part, in_g), (up_part, in_u), (down_part, in_d),
            )
        )
    ]
    outs = (o_q, o_k, o_v, o_o, o_g, o_u, o_d)
    loads = [
        pltpu.make_async_copy(a, b, lsem.at[k])
        for k, (a, b) in enumerate(
            (
                (qkv_heads, qkvh), (agh_in, agh), (att_heads, atth), (wq_in, wq),
                (wk_in, wk), (wv_in, wv), (xs_in, x),
            )
        )
    ]
    for ld in loads:
        ld.start()
    e.barrier()
    scat[6].start()
    scat[4].start()
    wide_t[...] = jnp.zeros_like(wide_t)
    for ld in loads[:3]:
        ld.wait()

    for s in range(seqs):
        acck[...] = jnp.zeros_like(acck)
        accv[...] = jnp.zeros_like(accv)
        for i in range(e.nc):
            keys = (i + 1) * span
            kb = qkvh[1, s, 0 : i + 1].reshape(keys, HD)
            vb = qkvh[2, s, 0 : i + 1].reshape(keys, HD)
            qb = qkvh[0, s, i]
            rowsl = pl.ds(i * span, span)
            scores = masked(dot(qb, kb, NT) * HD**-0.5, seg_col, seg_row, s, i, span)
            probs = jnp.exp(scores - lse[s, rowsl, 0:1])
            da = agh[s, i]
            accv[0:keys] += dot(probs.astype(BF), da, TN)
            delta = jnp.sum(da.astype(F32) * atth[s, i].astype(F32), axis=-1, keepdims=True)
            ds = (probs * (dot(da, vb, NT) - delta)).astype(BF)
            dh[0, s, i] = (dot(ds, kb, NN) * HD**-0.5).astype(BF)
            acck[0:keys] += dot(ds, qb, TN)
        dh[1, s] = (acck[...] * HD**-0.5).astype(BF).reshape(e.nc, span, HD)
        dh[2, s] = accv[...].astype(BF).reshape(e.nc, span, HD)
        own = pl.ds(pl.multiple_of(e.p * span, span), span)
        for k in range(3):
            dst = dx.at[k, s, lax.rem(e.c, heads), own, :]
            from_heads(e, dh.at[k, s], dst, dsend.at[k, s], drecv.at[k, s], heads)
    scat[5].start()
    scat[3].start()

    place = cut(e.t * 2 + e.p, wide)
    gmine[...] = gains_in[...]
    gmine[0:2, :] = jnp.zeros((2, dm), F32)
    inner = [[], []]
    for s in range(seqs):
        for k in range(3):
            wait_bytes(dx.at[k, s], drecv.at[k, s])
        for k, gain in enumerate((qgain, kgain)):
            for jj in range(heads):
                lanes = slice(jj * HD, (jj + 1) * HD)
                g = turn_back(dx[k, s, jj].astype(F32), angles[0, s], angles[1, s])
                uu[k, s, :, lanes] = g
            g = uu[k, s]
            unit = units[k, s]
            gmine[k : k + 1, place] += jnp.sum(g * unit, axis=0, keepdims=True)
            u = g * gain[:, place]
            uu[k, s] = u
            inner[k].append(jnp.sum(u * unit, axis=-1, keepdims=True))
        for jj in range(heads):
            pre[2, s, :, jj * HD : (jj + 1) * HD] = dx[2, s, jj]
    mine[...] = columns(*[jnp.concatenate(v, axis=0) for v in inner])
    ex = Exchange(e, mine, inbox, esem.at[0], esem.at[1], *Exchange.heads(e))
    ex.start()
    gx = Exchange(e, gmine, gin, g1sem.at[0], g1sem.at[1], *Exchange.plane(e))
    gx.start()
    for ld in loads[3:]:
        ld.wait()
    wide_t[0:8] = ex.finish() / D
    cols = wide_t[...].T
    for s in range(seqs):
        for k in range(2):
            mean = cols[s * 2 * span : (s + 1) * 2 * span, k : k + 1]
            v = scales[s][:, k : k + 1] * (uu[k, s] - units[k, s] * mean)
            pre[k, s] = v.astype(BF)

    tile = 512
    red = [
        Reduce(e, part.at[s], pair.at[s], right.at[s], left.at[s], rsem.at[s], rows)
        for s in range(seqs)
    ]
    for s in range(seqs):

        def step(i, s=s):
            sl = cut(i, tile)
            total = dot(pre[0, s], wq[sl, :], NT) + dot(pre[1, s], wk[sl, :], NT)
            part[s, :, sl] = (total + dot(pre[2, s], wv[sl, :], NT)).astype(BF)

        loop(dm // tile, step)
        red[s].pair_send()
    for s in range(seqs):
        red[s].pair_add()
        red[s].slot(-1)
    for k, w in enumerate((wq, wk, wv)):

        def step(i, k=k, w=w):
            sl = cut(i, tile)
            lhs = x[:, :, sl].reshape(-1, tile)
            w[sl, :] = dot(lhs, pre[k].reshape(-1, wide), TN).astype(BF)

        loop(dm // tile, step)
        scat[k].start()
        for s in range(seqs):
            red[s].slot(k)
    for j in range(3, n - 1):
        for s in range(seqs):
            red[s].slot(j)
    gmine[...] = gx.finish()
    gx2 = Exchange(e, gmine, gin2, g2sem.at[0], g2sem.at[1], *Exchange.line(e))
    gx2.start()
    for s in range(seqs):
        red[s].result(y)
        input_grad[s] = hidden_grad[s] + y[...]
    gains_out[...] = gx2.finish()

    stores = {}
    for turn_no, k in enumerate((6, 4, 5, 3, 0, 1, 2)):
        buf = turn_no % 2
        sc = scat[k]
        sc.wait()
        if buf in stores:
            stores[buf].wait()
        width = 2 * sc.half
        rb = sc.rows
        total = sc.inbox[0].astype(F32)
        for i in range(1, sc.inbox.shape[0]):
            total = total + sc.inbox[i].astype(F32)
        fin[buf, :, 0:width] = total
        stores[buf] = pltpu.make_async_copy(
            fin.at[buf, :, pl.ds(0, width)], outs[k], fsem.at[buf]
        )
        stores[buf].start()
    for st in stores.values():
        st.wait()
    for sc in scat:
        sc.drain()
    for s in range(seqs):
        red[s].drain()
        for k in range(3):
            from_heads_drain(e, dh.at[k, s], dsend.at[k, s], heads)


def tail_stage(sizes, *args):
    nf, nc, nt = sizes
    hidden_grad, xs, gate_part, wo_part = args[0], args[13], args[18], args[17]
    seqs, rows, dm = hidden_grad.shape
    half, wide = gate_part.shape[1], wo_part.shape[1]
    heads = wide // HD
    full = 2 * nt * rows
    span = nt * rows
    rb = dm // (nf * nc)
    slots = nf // 2 * nc
    sds = jax.ShapeDtypeStruct
    v, dma = pltpu.VMEM, pltpu.SemaphoreType.DMA
    small, large = v((slots, rb, 2 * wide), BF), v((slots, rb, 2 * half), BF)
    return pl.pallas_call(
        functools.partial(tail_kernel, sizes, seqs, rows),
        name="tail_stage",
        out_shape=(sds((seqs, rows, dm), F32), sds((8, dm), F32))
        + (sds((rb, 2 * wide), F32),) * 4
        + (sds((rb, 2 * half), F32),) * 3,
        in_specs=[VMEM_SPEC] * 10 + [HBM_SPEC] * 11,
        out_specs=(VMEM_SPEC,) * 2 + (HBM_SPEC,) * 7,
        scratch_shapes=[
            v((seqs, nc, span, HD), BF),
            v((3, seqs, nc, span, HD), BF),
            v((seqs, nc, span, HD), BF),
            v((seqs, full, dm), BF),
            v((dm, wide), BF),
            v((dm, wide), BF),
            v((dm, wide), BF),
            v((3, seqs, nc, span, HD), BF),
            v((3, seqs, heads, full, HD), BF),
            v((nc * span, HD), F32),
            v((nc * span, HD), F32),
            v((2, seqs, full, wide), F32),
            v((3, seqs, full, wide), BF),
            v((seqs, full, dm), BF),
            v((seqs, nt * rows, dm), BF),
            v((seqs, nt - 1, rows, dm), BF),
            v((seqs, nt - 1, rows, dm), BF),
            v((rows, dm), F32),
            v((8, seqs * full), F32),
            v((2 * nt, 8, seqs * full), F32),
            v((128, seqs * full), F32),
            v((8, dm), F32),
            v((nf * nc, 8, dm), F32),
            v((nt, 8, dm), F32),
            small, small, small, small, large, large, large,
            v((2, rb, 2 * half), F32),
            dma((7,)),
            dma((3, seqs, nc)),
            dma((3, seqs)),
            dma((2, 2 * nt)),
            dma((seqs, 4, nt)),
            dma((7, 2)),
            dma((2, nf * nc)),
            dma((2, nt)),
            dma((2,)),
        ],
        compiler_params=pltpu.CompilerParams(
            collective_id=3, has_side_effects=True, vmem_limit_bytes=63 << 20
        ),
    )(*args)


def body(
    tokens, segments, positions, query_weight, key_weight, value_weight, output_weight,
    gate_weight, up_projection_weight, down_weight, query_gain, key_gain, attention_gain,
    feedforward_gain, cotangent,
):
    sizes = (lax.axis_size("fsdp"), lax.axis_size("ctx"), lax.axis_size("tensor"))
    seqs, rows, _ = tokens.shape
    span = sizes[2] * rows
    block_pos = lax.dynamic_slice_in_dim(positions, lax.axis_index("ctx") * span, span, 1)
    cosine, sine = rope_tables(block_pos)
    cos_own = jnp.concatenate([cosine, cosine], axis=-1)
    sin_own = jnp.concatenate([-sine, sine], axis=-1)
    seg_col = segments[:, :, None]
    seg_row = segments[:, None, :]
    qgain, kgain = query_gain[None], key_gain[None]
    (
        att, xs, wq, wk, wv, units, scales, angles, qkv_heads, att_heads, lse,
    ) = front_stage(
        sizes, tokens, cos_own, sin_own, qgain, kgain, seg_col, seg_row,
        query_weight, key_weight, value_weight,
    )
    block_out, hidden_grad, agh, wo_part, gate_part, up_part, down_part, gains = ffn_stage(
        sizes, att, output_weight, gate_weight, up_projection_weight, down_weight,
        tokens, cotangent, attention_gain[None], feedforward_gain[None],
    )
    input_grad, gain_sums, *weight_grads = tail_stage(
        sizes, hidden_grad, gains, units, scales, angles, qgain, kgain, seg_col, seg_row, lse,
        agh, qkv_heads, att_heads, xs, wq, wk, wv, wo_part, gate_part, up_part, down_part,
    )
    return (block_out, input_grad, *weight_grads, *(gain_sums[k] for k in range(4)))


def solution(mesh):
    in_specs = (
        P("fsdp", ("ctx", "tensor"), None),
        P("fsdp", None),
        P("fsdp", None),
        P(("fsdp", "ctx"), "tensor"),
        P(("fsdp", "ctx"), "tensor"),
        P(("fsdp", "ctx"), "tensor"),
        P(("fsdp", "ctx"), "tensor"),
        P(("fsdp", "ctx"), "tensor"),
        P(("fsdp", "ctx"), "tensor"),
        P(("fsdp", "ctx"), "tensor"),
        P(),
        P(),
        P(),
        P(),
        P("fsdp", ("ctx", "tensor"), None),
    )
    out_specs = (
        P("fsdp", ("ctx", "tensor"), None),
        P("fsdp", ("ctx", "tensor"), None),
        P(("fsdp", "ctx"), "tensor"),
        P(("fsdp", "ctx"), "tensor"),
        P(("fsdp", "ctx"), "tensor"),
        P(("fsdp", "ctx"), "tensor"),
        P(("fsdp", "ctx"), "tensor"),
        P(("fsdp", "ctx"), "tensor"),
        P(("fsdp", "ctx"), "tensor"),
        P(),
        P(),
        P(),
        P(),
    )
    return jax.shard_map(body, mesh=mesh, in_specs=in_specs, out_specs=out_specs, check_vma=False)
```

time: 1520 us -> 624 us (0.41)
  waiting for transfers between devices: 1130 us -> 0 us
  Pallas kernels: 0 us -> 599 us
  matrix products: 159 us -> 0 us
  blocking collectives: 93.2 us -> 0 us
  local copies, waits for them, and re-layouts: 49.8 us -> 16 us
  other arithmetic: 35.7 us -> 2.69 us
  starting transfers between devices: 21.8 us -> 0 us
    reduce_scatter x11 -> x0, waiting for transfers between devices: 723 us -> none  [the longest x4 305 us: sum_tokens(): return lax.psum_scatter(terms, 'tensor', scatter_dimension=1, tiled=True)]
    pallas_call x0 -> x3, Pallas kernels: none -> 599 us  [the longest x1 307 us: ffn_stage(): pl.pallas_call(functools.partial(ffn_kernel, sizes, seqs, rows), name='ff...]
    all_gather x11 -> x0, waiting for transfers between devices: 377 us -> none  [the longest x4 184 us: gather_tokens(): return lax.all_gather(matrix_rows, 'tensor', axis=1, tiled=True)]
    dot_general x27 -> x0, matrix products: 159 us -> none  [the longest x7 48.6 us: project(): jnp.einsum('xmj,je->xme', matrix_rows, weight_matrix, preferred_element_t...]
    psum x3 -> x0, blocking collectives: 61 us -> none  [the longest x1 39.2 us: body(): lax.psum((query_gain_full, key_gain_full, attn_gain_grad, ffn_gain_grad),...]
    all_to_all x3 -> x0, blocking collectives: 32.1 us -> none  [the longest x1 11.8 us: body(): lax.all_to_all(heads_of(attended_output_gradient), 'ctx', split_axis=2, c...]
    all_to_all x5 -> x0, waiting for transfers between devices: 28.3 us -> none  [the longest x1 9.22 us: body(): lax.all_to_all(key_grad_heads, 'ctx', split_axis=1, concat_axis=2, tiled=...]
    all_to_all x5 -> x0, starting transfers between devices: 19.4 us -> none  [the longest x1 4.15 us: body(): lax.all_to_all(key_grad_heads, 'ctx', split_axis=1, concat_axis=2, tiled=...]
  transfers between devices with their start and end apart: 27 -> 0, of which waited for: 23 -> 0; matrix products, arithmetic and copies ran while one was open for 11% -> 0% of each run, Pallas kernels for 0% -> 0%
where the time goes in v1:
time: 624 us; the launch traced here: 619 us
  Pallas kernels  599 us (96%)
  local copies, waits for them, and re-layouts  16 us (3%)
    pallas_call x1, Pallas kernels, ffn_stage(): pl.pallas_call(functools.partial(ffn_kernel, sizes, seqs, rows), name='ff...  307 us
    pallas_call x1, Pallas kernels, tail_stage(): pl.pallas_call(functools.partial(tail_kernel, sizes, seqs, rows), name='t...  213 us
    pallas_call x1, Pallas kernels, front_stage(): pl.pallas_call(functools.partial(front_kernel, sizes, seqs, rows), name='...  78.6 us

profile of v1, /device:TPU:0, one launch (start us, length us, event | category | flops | bytes accessed | tf_op | source)
XLA Modules:
  0.0 618.5 jit_solution(18396491574088768748)
XLA Ops:
  0.6 0.0 copy-start.8
  0.7 0.7 dynamic-slice_convert_fusion
  1.4 1.0 fusion
  2.4 1.0 pad_maximum_fusion
  3.4 0.0 copy-done.8
  3.4 1.3 copy.28.seg_col
  4.7 0.6 broadcast_in_dim.23.seg_row
  5.3 78.6 %front_stage.1 = (bf16[2,512,256]{2,1,0:T(8,128)(2,1)}, bf16[2,512,2048]{2,1,0:T(8,128)(2,1)}, bf16[2048,256]{1,0:T(8,128)(2,1)}, bf16[2048,256]{1,0:T(8,128)(2,...) custom-call(bf16[2,64,2048]{2,1,0:T(8,128)(2,1)} %tokens.3, ...), custom_call_target="tpu_custom_call" | custom-call | tf_op jit(solution)/shard_map/front_stage/pallas_call | solution.py:896
  83.9 307.2 %ffn_stage.1 = (bf16[2,64,2048]{2,1,0:T(8,128)(2,1)}, f32[2,64,2048]{2,1,0:T(8,128)}, bf16[2,4,256,128]{3,2,1,0:T(8,128)(2,1)}, bf16[2048,256]{1,0:T(8,128)(2,1)...) custom-call(bf16[2,512,256]{2,1,0:T(8,128)(2,1)} %get-tuple-element., ...), custom_call_target="tpu_custom_call" | custom-call | tf_op jit(solution)/shard_map/ffn_stage/pallas_call | solution.py:612
  391.2 0.0 copy-start.3
  391.2 212.8 %tail_stage.1 = (f32[2,64,2048]{2,1,0:T(8,128)}, f32[8,2048]{1,0:T(8,128)}, f32[256,512]{1,0:T(8,128)}, f32[256,512]{1,0:T(8,128)}, f32[256,512]{1,0:T(8,128)}, ...) custom-call(f32[2,64,2048]{2,1,0:T(8,128)} %get-tuple-element.43.hidden_grad, ...), custom_call_target="tpu_custom_call" | custom-call | tf_op jit(solution)/shard_map/tail_stage/pallas_call | solution.py:1152
  604.0 0.0 copy-start.7
  604.0 1.7 fusion.1
  605.7 0.0 copy-done.3
  605.7 0.0 copy-start.6
  605.7 0.8 copy.39
  606.5 0.0 copy-start.5
  606.5 2.4 copy.40
  608.9 0.0 copy-done.7
  608.9 0.0 copy-start.4
  608.9 0.0 copy-start.2
  608.9 0.8 copy.41
  609.7 0.0 copy-done.6
  609.7 0.8 copy.42
  610.5 0.0 copy-done.5
  610.5 0.8 copy.43
  611.3 0.0 copy-done.4
  611.3 0.8 copy.44
  612.1 0.0 copy-done.2
  612.1 0.0 copy-start.1
  612.1 1.3 copy.45
  613.4 1.0 copy-done.1
  614.4 0.0 copy-start
  614.4 1.3 copy.46
  615.7 1.0 copy-done
  616.8 1.3 copy.47
  (1 shorter events, 0.0 us)
Async XLA Ops:
  0.6 2.7 copy-start.8
  391.2 214.6 %copy-start.3 = (bf16[2,64,2048]{2,1,0:T(8,128)(2,1)S(1)}, bf16[2,64,2048]{2,1,0:T(8,128)(2,1)}, u32[]{:S(2)}) copy-start(bf16[2,64,2048]{2,1,0:T(8,128)(2,1)} %get-tuple-element.91) | copy-start | bytes 1572868
  604.0 4.9 copy-start.7
  605.7 4.0 copy-start.6
  606.5 4.0 copy-start.5
  608.9 2.4 copy-start.4
  608.9 3.2 copy-start.2
  612.1 2.3 copy-start.1
  614.4 2.3 copy-start

commit v2 on v1

--- a/solution.py
+++ b/solution.py
@@ -286,48 +286,156 @@
 
 
 class Weight:
-    def __init__(self, e, shard, full, send, recv):
-        self.e, self.shard, self.full, self.send, self.recv = e, shard, full, send, recv
-        self.rows, self.half = shard.shape[0], full.shape[1]
+    def __init__(self, e, shard, full, sems, off=0):
+        self.e, self.shard, self.full, self.sems, self.off = e, shard, full, sems, off
+        self.rows, self.width = shard.shape[0], full.shape[1]
+        self.stride = shard.shape[1] // 2
+
+    def columns(self, core):
+        start = pl.multiple_of(core * self.stride + self.off, 128)
+        return self.shard.at[:, pl.ds(start, self.width)]
+
+    def some(self, count):
+        return self.full.at[pl.ds(0, count * self.rows), :]
+
+    def targets(self):
+        e = self.e
+        if e.nf == 2:
+            return [(0, 1, 0), (0, 2, 0), (0, 1, 1), (0, 2, 1), (0, 0, 1)]
+        return e.plane()
 
     def start(self):
         e = self.e
         dst = self.full.at[cut(e.f * e.nc + e.c, self.rows), :]
+        for off in self.targets():
+            f, core, c = e.peer(off)
+            remote(self.columns(core), dst, self.sems.at[0], self.sems.at[1], e.at(f=f, c=c)).start()
+        pltpu.make_async_copy(self.columns(e.p), dst, self.sems.at[1]).start()
+
+    def relay(self):
+        e = self.e
+        wait_bytes(self.some(len(self.targets()) + 1), self.sems.at[1])
+        if e.nf != 2:
+            return
+        part = self.rows // 2
+        for f in range(2):
+            for k, (source, target) in enumerate(((1, 2), (2, 1))):
+                row = (f * e.nc + jnp.bitwise_xor(e.c, source)) * self.rows + k * part
+                ref = self.full.at[pl.ds(pl.multiple_of(row, part), part), :]
+                device = e.at(c=jnp.bitwise_xor(e.c, target))
+                remote(ref, ref, self.sems.at[2], self.sems.at[3], device).start()
+
+    def wait(self):
+        if self.e.nf == 2:
+            wait_bytes(self.some(2), self.sems.at[3])
+
+    def drain(self):
+        wait_bytes(self.some(len(self.targets())), self.sems.at[0])
+        if self.e.nf == 2:
+            wait_bytes(self.some(2), self.sems.at[2])
+
+
+class Scatter:
+    def __init__(self, e, part, first, inbox, sems):
+        self.e, self.part, self.first, self.inbox, self.sems = e, part, first, inbox, sems
+        self.rows, self.half = inbox.shape[1], part.shape[1]
+        self.upper = self.rows // 2
+
+    def piece(self, f, c, side=None):
+        row = (f * self.e.nc + c) * self.rows
+        if side is None:
+            return self.part.at[pl.ds(pl.multiple_of(row, self.rows), self.rows), :]
+        row = pl.multiple_of(row + side * self.upper, self.upper)
+        return self.part.at[pl.ds(row, self.upper), :]
+
+    def start(self):
+        e = self.e
+        if e.nf == 2:
+            for side in range(2):
+                near = jnp.bitwise_xor(e.c, 1 + side)
+                for k, owner in enumerate((near, jnp.bitwise_xor(e.c, 3))):
+                    for f in range(2):
+                        remote(
+                            self.piece(f, owner, side), self.first.at[side, k, f],
+                            self.sems.at[0], self.sems.at[1], e.at(c=near),
+                        ).start()
+            return
+        slot = lax.div(e.group, 2) * e.nc + e.c
+        dst = self.inbox.at[slot, :, cut(e.p, self.half)]
         for off in e.plane():
-            f, core, c = e.peer(off)
+            f, _, c = e.peer(off)
             remote(
-                self.shard.at[:, cut(core, self.half)], dst, self.send, self.recv, e.at(f=f, c=c)
+                self.piece(f, c), dst, self.sems.at[2], self.sems.at[3], e.at(f=f, c=c)
             ).start()
-        pltpu.make_async_copy(self.shard.at[:, cut(e.p, self.half)], dst, self.recv).start()
+        pltpu.make_async_copy(self.piece(e.f, e.c), dst, self.sems.at[3]).start()
+
+    def relay(self):
+        e = self.e
+        if e.nf != 2:
+            return
+        wait_bytes(self.first, self.sems.at[1])
+        lanes = cut(e.p, self.half)
+        for side in range(2):
+            far = jnp.bitwise_xor(e.c, 2 - side)
+            for k, owner in enumerate((e.c, far)):
+                for f in range(2):
+                    mine = self.piece(f, owner, side)
+                    got = self.first[side, k, f].astype(F32)
+                    mine[...] = (mine[...].astype(F32) + got).astype(BF)
+            for f in range(2):
+                dst = self.inbox.at[1, pl.ds(side * self.upper, self.upper), lanes]
+                remote(
+                    self.piece(f, far, side), dst, self.sems.at[2], self.sems.at[3],
+                    e.at(f=f, c=far),
+                ).start()
+        dst = self.inbox.at[0, :, lanes]
+        remote(
+            self.piece(1 - e.p, e.c), dst, self.sems.at[2], self.sems.at[3], e.at(f=e.mate)
+        ).start()
+        pltpu.make_async_copy(self.piece(e.p, e.c), dst, self.sems.at[3]).start()
 
     def wait(self):
-        wait_bytes(self.full, self.recv)
+        wait_bytes(self.inbox, self.sems.at[3])
 
     def drain(self):
-        count = len(self.e.plane()) * self.rows
-        wait_bytes(self.full.at[pl.ds(0, count), :], self.send)
+        e = self.e
+        count = 3 if e.nf == 2 else len(e.plane())
+        wait_bytes(self.part.at[pl.ds(0, count * self.rows), :], self.sems.at[2])
+        if e.nf == 2:
+            wait_bytes(self.part.at[pl.ds(0, 4 * self.rows), :], self.sems.at[0])
+
+
+def scatter_shapes(sizes, dm, half):
+    nf, nc, _ = sizes
+    rb = dm // (nf * nc)
+    if nf == 2:
+        return (2, 2, 2, rb // 2, half), (2, rb, 2 * half)
+    return (1, 1, 1, 16, 128), (nf // 2 * nc, rb, 2 * half)
 
 
 def ffn_kernel(
     sizes, seqs, rows,
-    att, wo_sh, gate_sh, up_sh, down_sh, tokens, cot, again, fgain,
-    block_out, hidden_grad, agh, wo_part, gate_part, up_part, down_part, gains,
+    att, wo_in, gate_in, gate_sh, up_sh, down_sh, tokens, cot, again, fgain,
+    block_out, hidden_grad, agh, wo_part, gate_part, up_part, down_terms, gains,
     wo_v, g_v, u_v, d_v, part, pair, right, left, hid, mgr, agr, aa, bb, mixed,
-    unit1, hid32, scale1, scratch_y, agx,
-    wsem, rsem, gsem, xsend, xrecv, osem,
+    unit1, hid32, scale1, scratch_y, agx, first,
+    wsem, lsem, dsem, rsem, gsem, xsend, xrecv, osem,
 ):
     e = Place(*sizes)
     dm = tokens.shape[2]
     half = g_v.shape[1]
     wide = att.shape[2]
     heads = wide // HD
-    weights = [
-        Weight(e, sh, full, wsem.at[i, 0], wsem.at[i, 1])
-        for i, (sh, full) in enumerate(
-            ((wo_sh, wo_v), (gate_sh, g_v), (up_sh, u_v), (down_sh, d_v))
-        )
-    ]
-    w_o, w_g, w_u, w_d = weights
+    early = gate_in.shape[1]
+    late = g_v.at[:, pl.ds(early, half - early)]
+    w_g = Weight(e, gate_sh, late, wsem.at[0], off=early)
+    w_u = Weight(e, up_sh, u_v, wsem.at[1])
+    w_d = Weight(e, down_sh, d_v, wsem.at[2])
+    load_o = pltpu.make_async_copy(wo_in, wo_v, lsem.at[0])
+    load_g = pltpu.make_async_copy(gate_in, g_v.at[:, pl.ds(0, early)], lsem.at[1])
+    load_o.start()
+    load_g.start()
+    scat_d = Scatter(e, d_v, first, down_terms, dsem)
 
     def reduce(k, s):
         return Reduce(e, part.at[s], pair.at[s], right.at[s], left.at[s], rsem.at[k, s], rows)
@@ -339,8 +447,8 @@
     gat = [[gather(k, s) for s in range(seqs)] for k in range(3)]
 
     e.barrier()
-    for w in weights:
-        w.start()
+    w_g.start()
+    w_u.start()
     gains[...] = jnp.zeros_like(gains)
 
     tile = 512
@@ -471,7 +579,7 @@
                     lambda jj=jj, q=q: wait_bytes(block, xsend.at[s, jj, q]),
                 )
 
-    w_o.wait()
+    load_o.wait()
     out_tiles(0)
     red[0][0].pair_send()
     out_tiles(1)
@@ -490,10 +598,15 @@
         red[0][1].slot(i - 1)
         gat[0][0].slot(i - 1)
 
-    loop(n, step)
+    loop(2, step)
+    w_g.relay()
+    w_u.relay()
+    w_d.start()
+    loop(n - 2, lambda i: step(i + 2))
     gat[0][0].done()
     norm1(1)
     gat[0][1].init()
+    load_g.wait()
     w_g.wait()
     w_u.wait()
 
@@ -502,6 +615,7 @@
         gat[0][1].slot(i)
 
     loop(ffn_tiles, step)
+    w_d.relay()
     w_d.wait()
     red[0][0].drain()
     down_tiles(0)
@@ -555,32 +669,41 @@
     norm3(0)
     gat[2][0].init()
     red[2][1].pair_add()
+    red[2][1].slot(-1)
+    tiles = (dm // tile) * (half // tile)
+    share = -(-tiles // (n - 1))
+
+    def fill(left_rows, right_rows, out, i):
+        def go(k):
+            which = share * i + k
+            when(which < tiles, lambda: weight_tile(left_rows, right_rows, out, which, tile))
+
+        loop(share, go)
+
+    for w in (w_g, w_u, w_d):
+        w.drain()
+    loop(tiles, lambda i: weight_tile(mgr, mixed, d_v, i, tile))
+    scat_d.start()
 
     def step(i):
-        red[2][1].slot(i - 1)
-        gat[2][0].slot(i - 1)
-
-        def fill(k):
-            weight_tile(mgr, mixed, d_v, 2 * i + k, tile)
-            weight_tile(hid, aa, g_v, 2 * i + k, tile)
-
-        loop(2, fill)
-
-    loop(n, step)
-    out_d = pltpu.make_async_copy(d_v, down_part, osem.at[0])
+        red[2][1].slot(i)
+        gat[2][0].slot(i)
+        fill(hid, aa, g_v, i)
+
+    loop(n - 1, step)
     out_g = pltpu.make_async_copy(g_v, gate_part, osem.at[1])
-    out_d.start()
     out_g.start()
     norm3(1)
     gat[2][1].init()
     gat[2][0].done()
     heads_grad(0)
+    scat_d.relay()
 
     def step(i):
-        gat[2][1].slot(i - 1)
-        loop(2, lambda k: weight_tile(hid, bb, u_v, 2 * i + k, tile))
-
-    loop(n, step)
+        gat[2][1].slot(i)
+        fill(hid, bb, u_v, i)
+
+    loop(n - 1, step)
     out_u = pltpu.make_async_copy(u_v, up_part, osem.at[2])
     out_u.start()
     gat[2][1].done()
@@ -595,17 +718,20 @@
     for k in range(3):
         for s in range(seqs):
             gat[k][s].drain()
-    for w in weights:
-        w.drain()
-    for o in (out_d, out_g, out_u, out_o):
+    scat_d.wait()
+    scat_d.drain()
+    for o in (out_g, out_u, out_o):
         o.wait()
 
 
-def ffn_stage(sizes, att, wo_sh, gate_sh, up_sh, down_sh, tokens, cot, again, fgain):
+def ffn_stage(
+    sizes, att, wo_in, gate_in, gate_sh, up_sh, down_sh, tokens, cot, again, fgain
+):
     nf, nc, nt = sizes
     seqs, rows, dm = tokens.shape
     half = gate_sh.shape[1] // 2
-    wide = wo_sh.shape[1] // 2
+    wide = wo_in.shape[1]
+    first, terms = scatter_shapes(sizes, dm, half)
     full = 2 * nt * rows
     sds = jax.ShapeDtypeStruct
     v, dma = pltpu.VMEM, pltpu.SemaphoreType.DMA
@@ -619,10 +745,10 @@
             sds((dm, wide), BF),
             sds((dm, half), BF),
             sds((dm, half), BF),
-            sds((dm, half), BF),
+            sds(terms, BF),
             sds((8, dm), F32),
         ),
-        in_specs=[VMEM_SPEC] + [HBM_SPEC] * 4 + [VMEM_SPEC] * 4,
+        in_specs=[VMEM_SPEC] + [HBM_SPEC] * 5 + [VMEM_SPEC] * 4,
         out_specs=(VMEM_SPEC, VMEM_SPEC) + (HBM_SPEC,) * 5 + (VMEM_SPEC,),
         scratch_shapes=[
             v((dm, wide), BF),
@@ -644,7 +770,10 @@
             v((seqs, rows, 128), F32),
             v((rows, dm), F32),
             v((seqs, wide // HD, full, HD), BF),
-            dma((4, 2)),
+            v(first, BF),
+            dma((3, 4)),
+            dma((2,)),
+            dma((4,)),
             dma((3, seqs, 4, nt)),
             dma((3, seqs, 6, 2 * nt - 1)),
             dma((seqs, wide // HD, 2)),
@@ -654,7 +783,7 @@
         compiler_params=pltpu.CompilerParams(
             collective_id=1, has_side_effects=True, vmem_limit_bytes=63 << 20
         ),
-    )(att, wo_sh, gate_sh, up_sh, down_sh, tokens, cot, again, fgain)
+    )(att, wo_in, gate_in, gate_sh, up_sh, down_sh, tokens, cot, again, fgain)
 
 
 class Exchange:
@@ -773,8 +902,8 @@
 
 def front_kernel(
     sizes, seqs, rows,
-    tokens, cos_own, sin_own, qgain, kgain, seg_col, seg_row, wq_sh, wk_sh, wv_sh,
-    att, xs_out, wq_out, wk_out, wv_out, units, scales, angles, qkv_heads, att_heads, lse,
+    tokens, cos_own, sin_own, qgain, kgain, seg_col, seg_row, wq_sh, wk_sh, wv_sh, wo_sh, gate_sh,
+    att, xs_out, wq_out, wk_out, wv_out, wo_out, gate_out, units, scales, angles, qkv_heads, att_heads, lse,
     x, wq, wk, wv, lin, qkvx, qkvh, atth, mine, inbox, wide_t, ang,
     wsem, gsem, asem, esem, hsend, hrecv, bsend, brecv, osem,
 ):
@@ -783,10 +912,8 @@
     span = n * rows
     wide = wq.shape[1]
     heads = wide // HD
-    ws = [
-        Weight(e, sh, full, wsem.at[i, 0], wsem.at[i, 1])
-        for i, (sh, full) in enumerate(((wq_sh, wq), (wk_sh, wk), (wv_sh, wv)))
-    ]
+    pairs = ((wq_sh, wq), (wk_sh, wk), (wv_sh, wv), (wo_sh, wo_out), (gate_sh, gate_out))
+    ws = [Weight(e, sh, full, wsem.at[i]) for i, (sh, full) in enumerate(pairs)]
     gat = [Gather(e, x.at[s], gsem.at[s], rows) for s in range(seqs)]
     own = pl.ds(pl.multiple_of(e.p * span, span), span)
 
@@ -809,7 +936,12 @@
         for s in range(seqs):
             gat[s].slot(j)
 
-    loop(n - 1, step)
+    loop(n - 2, step)
+    for w in (ws[2], ws[0], ws[1]):
+        w.relay()
+    ws[3].start()
+    ws[4].start()
+    step(n - 2)
     for s in range(seqs):
         gat[s].done()
     outs = [pltpu.make_async_copy(x, xs_out, osem.at[0])]
@@ -851,6 +983,9 @@
                 qkvx[k, s, jj] = turned.astype(BF)
             to_heads(e, qkvx.at[k, s], qkvh.at[k, s], hsend.at[k, s], hrecv.at[k, s], heads, span)
 
+    ws[3].relay()
+    ws[4].relay()
+
     for s in range(seqs):
         for k in (2, 0, 1):
             wait_bytes(qkvh.at[k, s], hrecv.at[k, s])
@@ -878,13 +1013,17 @@
             to_heads_drain(e, qkvx.at[k, s], hsend.at[k, s], heads, span)
         gat[s].drain()
     angle_copy().wait_send()
+    ws[3].wait()
+    ws[4].wait()
     for w in ws:
         w.drain()
     for o in outs:
         o.wait()
 
 
-def front_stage(sizes, tokens, cos_own, sin_own, qgain, kgain, seg_col, seg_row, wq, wk, wv):
+def front_stage(
+    sizes, tokens, cos_own, sin_own, qgain, kgain, seg_col, seg_row, wq, wk, wv, wo, gate
+):
     nf, nc, nt = sizes
     seqs, rows, dm = tokens.shape
     wide = wq.shape[1] // 2
@@ -902,6 +1041,8 @@
             sds((dm, wide), BF),
             sds((dm, wide), BF),
             sds((dm, wide), BF),
+            sds((dm, wide), BF),
+            sds((dm, gate.shape[1] // 4), BF),
             sds((2, seqs, full, wide), F32),
             sds((seqs, full, 128), F32),
             sds((2, seqs, full, HD), F32),
@@ -909,8 +1050,8 @@
             sds((seqs, nc, span, HD), BF),
             sds((seqs, nc * span, HD), F32),
         ),
-        in_specs=[VMEM_SPEC] * 7 + [HBM_SPEC] * 3,
-        out_specs=(HBM_SPEC,) * 5 + (VMEM_SPEC,) * 3 + (HBM_SPEC,) * 2 + (VMEM_SPEC,),
+        in_specs=[VMEM_SPEC] * 7 + [HBM_SPEC] * 5,
+        out_specs=(HBM_SPEC,) * 7 + (VMEM_SPEC,) * 3 + (HBM_SPEC,) * 2 + (VMEM_SPEC,),
         scratch_shapes=[
             v((seqs, full, dm), BF),
             v((dm, wide), BF),
@@ -924,7 +1065,7 @@
             v((2 * nt, 8, seqs * full), F32),
             v((128, seqs * full), F32),
             v((2, seqs, full, HD), F32),
-            dma((3, 2)),
+            dma((5, 4)),
             dma((seqs, 6, 2 * nt - 1)),
             dma((2,)),
             dma((2, 2 * nt)),
@@ -937,43 +1078,18 @@
         compiler_params=pltpu.CompilerParams(
             collective_id=2, has_side_effects=True, vmem_limit_bytes=60 << 20
         ),
-    )(tokens, cos_own, sin_own, qgain, kgain, seg_col, seg_row, wq, wk, wv)
-
-
-class Scatter:
-    def __init__(self, e, part, inbox, send, recv):
-        self.e, self.part, self.inbox, self.send, self.recv = e, part, inbox, send, recv
-        self.rows, self.half = inbox.shape[1], part.shape[1]
-
-    def piece(self, f, c):
-        return self.part.at[cut(f * self.e.nc + c, self.rows), :]
-
-    def start(self):
-        e = self.e
-        slot = lax.div(e.group, 2) * e.nc + e.c
-        dst = self.inbox.at[slot, :, cut(e.p, self.half)]
-        for off in e.plane():
-            f, _, c = e.peer(off)
-            remote(self.piece(f, c), dst, self.send, self.recv, e.at(f=f, c=c)).start()
-        pltpu.make_async_copy(self.piece(e.f, e.c), dst, self.recv).start()
-
-    def wait(self):
-        wait_bytes(self.inbox, self.recv)
-
-    def drain(self):
-        count = len(self.e.plane()) * self.rows
-        wait_bytes(self.part.at[pl.ds(0, count), :], self.send)
+    )(tokens, cos_own, sin_own, qgain, kgain, seg_col, seg_row, wq, wk, wv, wo, gate)
 
 
 def tail_kernel(
     sizes, seqs, rows,
     hidden_grad, gains_in, units, scales, angles, qgain, kgain, seg_col, seg_row, lse,
     agh_in, qkv_heads, att_heads, xs_in, wq_in, wk_in, wv_in,
-    wo_part, gate_part, up_part, down_part,
-    input_grad, gains_out, o_q, o_k, o_v, o_o, o_g, o_u, o_d,
+    wo_part, gate_part, up_part,
+    input_grad, gains_out, in_q, in_k, in_v, in_o, in_g, in_u,
     agh, qkvh, atth, x, wq, wk, wv, dh, dx, acck, accv, uu, pre, part, pair, right, left, y,
-    mine, inbox, wide_t, gmine, gin, gin2, in_q, in_k, in_v, in_o, in_g, in_u, in_d, fin,
-    lsem, dsend, drecv, esem, rsem, ssem, g1sem, g2sem, fsem,
+    mine, inbox, wide_t, gmine, gin, gin2, p_o, p_g, p_u, f_q, f_k, f_v, f_o, f_g, f_u,
+    lsem, dsend, drecv, esem, rsem, ssem, g1sem, g2sem,
 ):
     e = Place(*sizes)
     n = e.nt
@@ -982,29 +1098,31 @@
     wide = wq.shape[1]
     heads = wide // HD
     scat = [
-        Scatter(e, p, b, ssem.at[k, 0], ssem.at[k, 1])
-        for k, (p, b) in enumerate(
+        Scatter(e, p, fi, b, ssem.at[k])
+        for k, (p, fi, b) in enumerate(
             (
-                (wq, in_q), (wk, in_k), (wv, in_v), (wo_part, in_o),
-                (gate_part, in_g), (up_part, in_u), (down_part, in_d),
+                (wq, f_q, in_q), (wk, f_k, in_k), (wv, f_v, in_v),
+                (p_o, f_o, in_o), (p_g, f_g, in_g), (p_u, f_u, in_u),
             )
         )
     ]
-    outs = (o_q, o_k, o_v, o_o, o_g, o_u, o_d)
     loads = [
         pltpu.make_async_copy(a, b, lsem.at[k])
         for k, (a, b) in enumerate(
             (
                 (qkv_heads, qkvh), (agh_in, agh), (att_heads, atth), (wq_in, wq),
                 (wk_in, wk), (wv_in, wv), (xs_in, x),
+                (gate_part, p_g), (wo_part, p_o), (up_part, p_u),
             )
         )
     ]
     for ld in loads:
         ld.start()
     e.barrier()
-    scat[6].start()
+    loads[7].wait()
     scat[4].start()
+    loads[8].wait()
+    scat[3].start()
     wide_t[...] = jnp.zeros_like(wide_t)
     for ld in loads[:3]:
         ld.wait()
@@ -1032,8 +1150,10 @@
         for k in range(3):
             dst = dx.at[k, s, lax.rem(e.c, heads), own, :]
             from_heads(e, dh.at[k, s], dst, dsend.at[k, s], drecv.at[k, s], heads)
+    scat[4].relay()
+    scat[3].relay()
+    loads[9].wait()
     scat[5].start()
-    scat[3].start()
 
     place = cut(e.t * 2 + e.p, wide)
     gmine[...] = gains_in[...]
@@ -1060,7 +1180,7 @@
     ex.start()
     gx = Exchange(e, gmine, gin, g1sem.at[0], g1sem.at[1], *Exchange.plane(e))
     gx.start()
-    for ld in loads[3:]:
+    for ld in loads[3:7]:
         ld.wait()
     wide_t[0:8] = ex.finish() / D
     cols = wide_t[...].T
@@ -1098,37 +1218,22 @@
         scat[k].start()
         for s in range(seqs):
             red[s].slot(k)
+        if k == 0:
+            scat[5].relay()
     for j in range(3, n - 1):
         for s in range(seqs):
             red[s].slot(j)
     gmine[...] = gx.finish()
     gx2 = Exchange(e, gmine, gin2, g2sem.at[0], g2sem.at[1], *Exchange.line(e))
     gx2.start()
+    for k in range(3):
+        scat[k].relay()
     for s in range(seqs):
         red[s].result(y)
         input_grad[s] = hidden_grad[s] + y[...]
     gains_out[...] = gx2.finish()
-
-    stores = {}
-    for turn_no, k in enumerate((6, 4, 5, 3, 0, 1, 2)):
-        buf = turn_no % 2
-        sc = scat[k]
+    for sc in scat:
         sc.wait()
-        if buf in stores:
-            stores[buf].wait()
-        width = 2 * sc.half
-        rb = sc.rows
-        total = sc.inbox[0].astype(F32)
-        for i in range(1, sc.inbox.shape[0]):
-            total = total + sc.inbox[i].astype(F32)
-        fin[buf, :, 0:width] = total
-        stores[buf] = pltpu.make_async_copy(
-            fin.at[buf, :, pl.ds(0, width)], outs[k], fsem.at[buf]
-        )
-        stores[buf].start()
-    for st in stores.values():
-        st.wait()
-    for sc in scat:
         sc.drain()
     for s in range(seqs):
         red[s].drain()
@@ -1144,19 +1249,18 @@
     heads = wide // HD
     full = 2 * nt * rows
     span = nt * rows
-    rb = dm // (nf * nc)
-    slots = nf // 2 * nc
     sds = jax.ShapeDtypeStruct
     v, dma = pltpu.VMEM, pltpu.SemaphoreType.DMA
-    small, large = v((slots, rb, 2 * wide), BF), v((slots, rb, 2 * half), BF)
+    small, small_terms = scatter_shapes(sizes, dm, wide)
+    large, large_terms = scatter_shapes(sizes, dm, half)
     return pl.pallas_call(
         functools.partial(tail_kernel, sizes, seqs, rows),
         name="tail_stage",
         out_shape=(sds((seqs, rows, dm), F32), sds((8, dm), F32))
-        + (sds((rb, 2 * wide), F32),) * 4
-        + (sds((rb, 2 * half), F32),) * 3,
-        in_specs=[VMEM_SPEC] * 10 + [HBM_SPEC] * 11,
-        out_specs=(VMEM_SPEC,) * 2 + (HBM_SPEC,) * 7,
+        + (sds(small_terms, BF),) * 4
+        + (sds(large_terms, BF),) * 2,
+        in_specs=[VMEM_SPEC] * 10 + [HBM_SPEC] * 10,
+        out_specs=(VMEM_SPEC,) * 2 + (HBM_SPEC,) * 6,
         scratch_shapes=[
             v((seqs, nc, span, HD), BF),
             v((3, seqs, nc, span, HD), BF),
@@ -1182,17 +1286,23 @@
             v((8, dm), F32),
             v((nf * nc, 8, dm), F32),
             v((nt, 8, dm), F32),
-            small, small, small, small, large, large, large,
-            v((2, rb, 2 * half), F32),
-            dma((7,)),
+            v((dm, wide), BF),
+            v((dm, half), BF),
+            v((dm, half), BF),
+            v(small, BF),
+            v(small, BF),
+            v(small, BF),
+            v(small, BF),
+            v(large, BF),
+            v(large, BF),
+            dma((10,)),
             dma((3, seqs, nc)),
             dma((3, seqs)),
             dma((2, 2 * nt)),
             dma((seqs, 4, nt)),
-            dma((7, 2)),
+            dma((6, 4)),
             dma((2, nf * nc)),
             dma((2, nt)),
-            dma((2,)),
         ],
         compiler_params=pltpu.CompilerParams(
             collective_id=3, has_side_effects=True, vmem_limit_bytes=63 << 20
@@ -1216,19 +1326,20 @@
     seg_row = segments[:, None, :]
     qgain, kgain = query_gain[None], key_gain[None]
     (
-        att, xs, wq, wk, wv, units, scales, angles, qkv_heads, att_heads, lse,
+        att, xs, wq, wk, wv, wo, gate, units, scales, angles, qkv_heads, att_heads, lse,
     ) = front_stage(
         sizes, tokens, cos_own, sin_own, qgain, kgain, seg_col, seg_row,
-        query_weight, key_weight, value_weight,
+        query_weight, key_weight, value_weight, output_weight, gate_weight,
     )
-    block_out, hidden_grad, agh, wo_part, gate_part, up_part, down_part, gains = ffn_stage(
-        sizes, att, output_weight, gate_weight, up_projection_weight, down_weight,
+    block_out, hidden_grad, agh, wo_part, gate_part, up_part, down_terms, gains = ffn_stage(
+        sizes, att, wo, gate, gate_weight, up_projection_weight, down_weight,
         tokens, cotangent, attention_gain[None], feedforward_gain[None],
     )
-    input_grad, gain_sums, *weight_grads = tail_stage(
+    input_grad, gain_sums, *terms = tail_stage(
         sizes, hidden_grad, gains, units, scales, angles, qgain, kgain, seg_col, seg_row, lse,
-        agh, qkv_heads, att_heads, xs, wq, wk, wv, wo_part, gate_part, up_part, down_part,
+        agh, qkv_heads, att_heads, xs, wq, wk, wv, wo_part, gate_part, up_part,
     )
+    weight_grads = [jnp.sum(x.astype(F32), axis=0) for x in (*terms, down_terms)]
     return (block_out, input_grad, *weight_grads, *(gain_sums[k] for k in range(4)))
 
 

time: 624 us -> 505 us (0.81)
  Pallas kernels: 599 us -> 478 us
  other arithmetic: 2.69 us -> 13.8 us
  local copies, waits for them, and re-layouts: 16 us -> 6.53 us
    pallas_call x1, Pallas kernels: 213 us -> 136 us  [tail_stage(): pl.pallas_call(functools.partial(tail_kernel, sizes, seqs, rows), name='t...]
    pallas_call x1, Pallas kernels: 307 us -> 250 us  [ffn_stage(): pl.pallas_call(functools.partial(ffn_kernel, sizes, seqs, rows), name='ff...]
    pallas_call x1, Pallas kernels: 78.6 us -> 91.9 us  [front_stage(): pl.pallas_call(functools.partial(front_kernel, sizes, seqs, rows), name='...]
    reduce_sum x0 -> x7, other arithmetic: none -> 11.1 us  [body(): jnp.sum(x.astype(F32), axis=0)]
    unnamed x27 -> x18, local copies, waits for them, and re-layouts: 12.4 us -> 2.23 us
where the time goes in v2:
time: 505 us; the launch traced here: 499 us
  Pallas kernels  478 us (95%)
  other arithmetic  13.8 us (3%)
  local copies, waits for them, and re-layouts  6.53 us (1%)
    pallas_call x1, Pallas kernels, ffn_stage(): pl.pallas_call(functools.partial(ffn_kernel, sizes, seqs, rows), name='ff...  250 us
    pallas_call x1, Pallas kernels, tail_stage(): pl.pallas_call(functools.partial(tail_kernel, sizes, seqs, rows), name='t...  136 us
    pallas_call x1, Pallas kernels, front_stage(): pl.pallas_call(functools.partial(front_kernel, sizes, seqs, rows), name='...  91.9 us
    reduce_sum x7, other arithmetic, body(): jnp.sum(x.astype(F32), axis=0)  11.1 us

profile of v2, /device:TPU:0, one launch (start us, length us, event | category | flops | bytes accessed | tf_op | source)
XLA Modules:
  0.0 499.0 jit_solution(12318141988688139382)
XLA Ops:
  0.6 0.0 copy-start.7
  0.7 0.7 dynamic-slice_convert_fusion
  1.4 1.3 broadcast_in_dim.23.seg_row
  2.7 1.0 fusion
  3.7 1.0 pad_maximum_fusion
  4.7 0.0 copy-done.7
  4.7 1.3 copy.28.seg_col
  6.0 91.9 %front_stage.1 = (bf16[2,512,256]{2,1,0:T(8,128)(2,1)}, bf16[2,512,2048]{2,1,0:T(8,128)(2,1)}, bf16[2048,256]{1,0:T(8,128)(2,1)}, bf16[2048,256]{1,0:T(8,128)(2,...) custom-call(bf16[2,64,2048]{2,1,0:T(8,128)(2,1)} %tokens.3, ...), custom_call_target="tpu_custom_call" | custom-call | tf_op jit(solution)/shard_map/front_stage/pallas_call | solution.py:1035
  97.9 250.1 %ffn_stage.1 = (bf16[2,64,2048]{2,1,0:T(8,128)(2,1)}, f32[2,64,2048]{2,1,0:T(8,128)}, bf16[2,4,256,128]{3,2,1,0:T(8,128)(2,1)}, bf16[2048,256]{1,0:T(8,128)(2,1)...) custom-call(bf16[2,512,256]{2,1,0:T(8,128)(2,1)} %get-tuple-element., ...), custom_call_target="tpu_custom_call" | custom-call | tf_op jit(solution)/shard_map/ffn_stage/pallas_call | solution.py:738
  348.0 135.8 %tail_stage.1 = (f32[2,64,2048]{2,1,0:T(8,128)}, f32[8,2048]{1,0:T(8,128)}, bf16[2,256,512]{2,1,0:T(8,128)(2,1)}, bf16[2,256,512]{2,1,0:T(8,128)(2,1)}, bf16[2,2...) custom-call(f32[2,64,2048]{2,1,0:T(8,128)} %get-tuple-element.46.hid, ...), custom_call_target="tpu_custom_call" | custom-call | tf_op jit(solution)/shard_map/tail_stage/pallas_call | solution.py:1256
  483.8 0.0 copy-start.6
  483.8 0.0 copy-start.5
  483.8 1.6 fusion.1
  485.5 0.0 copy-start.2
  485.5 2.1 convert_reduce_fusion.6
  487.6 2.0 convert_reduce_fusion.5
  489.5 0.0 copy-done.6
  489.5 0.9 convert_reduce_fusion.4
  490.4 0.0 copy-done.5
  490.4 0.9 convert_reduce_fusion.3
  491.3 0.0 copy-done.2
  491.3 0.0 copy-start.1
  491.3 1.8 convert_reduce_fusion.2
  493.1 0.2 copy-done.1
  493.3 0.0 copy-start
  493.3 1.8 convert_reduce_fusion.1
  495.0 0.2 copy-done
  495.3 0.0 copy-start.4
  495.3 0.0 copy-start.3
  495.3 1.8 convert_reduce_fusion
  497.0 0.0 copy-done.4
  497.0 0.8 copy.32
  497.8 0.0 copy-done.3
  497.8 1.0 copy.33
  (1 shorter events, 0.0 us)
Async XLA Ops:
  0.6 4.0 copy-start.7
  483.8 5.7 %copy-start.6 = (bf16[2,256,512]{2,1,0:T(8,128)(2,1)S(1)}, bf16[2,256,512]{2,1,0:T(8,128)(2,1)}, u32[]{:S(2)}) copy-start(bf16[2,256,512]{2,1,0:T(8,128)(2,1)} %get-tuple-element.65) | copy-start | bytes 1572868
  483.8 6.6 %copy-start.5 = (bf16[2,256,512]{2,1,0:T(8,128)(2,1)S(1)}, bf16[2,256,512]{2,1,0:T(8,128)(2,1)}, u32[]{:S(2)}) copy-start(bf16[2,256,512]{2,1,0:T(8,128)(2,1)} %get-tuple-element.66) | copy-start | bytes 1572868
  485.5 5.8 %copy-start.2 = (bf16[2,256,2048]{2,1,0:T(8,128)(2,1)S(1)}, bf16[2,256,2048]{2,1,0:T(8,128)(2,1)}, u32[]{:S(2)}) copy-start(bf16[2,256,2048]{2,1,0:T(8,128)(2,1)} %get-tuple-element.67) | copy-start | bytes 6291460
  491.3 2.0 copy-start.1
  493.3 2.0 copy-start
  495.3 1.8 copy-start.4
  495.3 2.6 copy-start.3

commit v3 on v2

--- a/solution.py
+++ b/solution.py
@@ -283,6 +283,26 @@
                 both(e.t + 1 + j <= n - 1, e.t > 0),
                 lambda j=j: self._side(e.t + 1 + j, j + 1, False).wait_send(),
             )
+
+
+SPLIT = 2
+
+
+def parts_of(width):
+    size = width // SPLIT
+    return [pl.ds(u * size, size) for u in range(SPLIT)]
+
+
+class Both:
+    def __init__(self, each):
+        self.each = list(each)
+
+    def __getattr__(self, name):
+        def call(*args):
+            for x in self.each:
+                getattr(x, name)(*args)
+
+        return call
 
 
 class Weight:
@@ -416,9 +436,9 @@
 def ffn_kernel(
     sizes, seqs, rows,
     att, wo_in, gate_in, gate_sh, up_sh, down_sh, tokens, cot, again, fgain,
-    block_out, hidden_grad, agh, wo_part, gate_part, up_part, down_terms, gains,
+    block_out, hidden_grad, agh, wo_part, gate_terms, up_part, down_terms, gains,
     wo_v, g_v, u_v, d_v, part, pair, right, left, hid, mgr, agr, aa, bb, mixed,
-    unit1, hid32, scale1, scratch_y, agx, first,
+    unit1, hid32, scale1, scratch_y, agx, first, first_g,
     wsem, lsem, dsem, rsem, gsem, xsend, xrecv, osem,
 ):
     e = Place(*sizes)
@@ -435,13 +455,31 @@
     load_g = pltpu.make_async_copy(gate_in, g_v.at[:, pl.ds(0, early)], lsem.at[1])
     load_o.start()
     load_g.start()
-    scat_d = Scatter(e, d_v, first, down_terms, dsem)
+    scat_d = Scatter(e, d_v, first, down_terms, dsem.at[0])
+    scat_g = Scatter(e, g_v, first_g, gate_terms, dsem.at[1])
 
     def reduce(k, s):
-        return Reduce(e, part.at[s], pair.at[s], right.at[s], left.at[s], rsem.at[k, s], rows)
+        return Both(
+            Reduce(
+                e, part.at[s, :, cl], pair.at[s, :, cl], right.at[s, :, :, cl],
+                left.at[s, :, :, cl], rsem.at[k, s, u], rows,
+            )
+            for u, cl in enumerate(parts_of(dm))
+        )
 
     def gather(k, s):
-        return Gather(e, (hid, mgr, agr)[k].at[s], gsem.at[k, s], rows)
+        full = (hid, mgr, agr)[k]
+        return Both(
+            Gather(e, full.at[s, :, cl], gsem.at[k, s, u], rows)
+            for u, cl in enumerate(parts_of(dm))
+        )
+
+    def own_rows(k, s):
+        return (hid, mgr, agr)[k].at[s, cut(e.p * e.nt + e.t, rows), :]
+
+    def result(k, s, out):
+        for r, cl in zip(red[k][s].each, parts_of(dm)):
+            r.result(out.at[:, cl])
 
     red = [[reduce(k, s) for s in range(seqs)] for k in range(3)]
     gat = [[gather(k, s) for s in range(seqs)] for k in range(3)]
@@ -462,7 +500,7 @@
 
     def norm1(s):
         y = scratch_y
-        red[0][s].result(y)
+        result(0, s, y)
         v = y[...]
         scale = lax.rsqrt(jnp.mean(v * v, axis=-1, keepdims=True) + epsilon)
         unit = v * scale
@@ -470,7 +508,7 @@
         scale1[s] = jnp.broadcast_to(scale, scale1.shape[1:])
         h = tokens[s].astype(F32) + unit * again[...]
         hid32[s] = h
-        gat[0][s].block(e.p, e.t)[...] = h.astype(BF)
+        own_rows(0, s)[...] = h.astype(BF)
 
     def ffn_tile(s, i):
         sl = cut(i, 256)
@@ -493,7 +531,7 @@
 
     def norm2(s):
         y = scratch_y
-        red[1][s].result(y)
+        result(1, s, y)
         v = y[...]
         scale = lax.rsqrt(jnp.mean(v * v, axis=-1, keepdims=True) + epsilon)
         unit = v * scale
@@ -502,7 +540,7 @@
         gains[3:4, :] += jnp.sum(upstream * unit, axis=0, keepdims=True)
         g = upstream * fgain[...]
         m = scale * (g - unit * jnp.mean(g * unit, axis=-1, keepdims=True))
-        gat[1][s].block(e.p, e.t)[...] = m.astype(BF)
+        own_rows(1, s)[...] = m.astype(BF)
 
     def inner_tiles(s):
         def step(i):
@@ -522,7 +560,7 @@
 
     def norm3(s):
         y = scratch_y
-        red[2][s].result(y)
+        result(2, s, y)
         hg = cot[s].astype(F32) + y[...]
         hidden_grad[s] = hg
         unit = unit1[s]
@@ -530,7 +568,7 @@
         g = hg * again[...]
         scale = scale1[s][:, 0:1]
         a = scale * (g - unit * jnp.mean(g * unit, axis=-1, keepdims=True))
-        gat[2][s].block(e.p, e.t)[...] = a.astype(BF)
+        own_rows(2, s)[...] = a.astype(BF)
 
     def weight_tile(left_rows, right_rows, out, i, width):
         per = out.shape[1] // width
@@ -691,8 +729,7 @@
         fill(hid, aa, g_v, i)
 
     loop(n - 1, step)
-    out_g = pltpu.make_async_copy(g_v, gate_part, osem.at[1])
-    out_g.start()
+    scat_g.start()
     norm3(1)
     gat[2][1].init()
     gat[2][0].done()
@@ -708,6 +745,7 @@
     out_u.start()
     gat[2][1].done()
     heads_grad(1)
+    scat_g.relay()
     loop(dm // tile, lambda i: weight_tile(agr, att, wo_v, i, wide))
     out_o = pltpu.make_async_copy(wo_v, wo_part, osem.at[3])
     out_o.start()
@@ -718,9 +756,10 @@
     for k in range(3):
         for s in range(seqs):
             gat[k][s].drain()
-    scat_d.wait()
-    scat_d.drain()
-    for o in (out_g, out_u, out_o):
+    for sc in (scat_d, scat_g):
+        sc.wait()
+        sc.drain()
+    for o in (out_u, out_o):
         o.wait()
 
 
@@ -743,7 +782,7 @@
             sds((seqs, rows, dm), F32),
             sds((seqs, nc, nt * rows, HD), BF),
             sds((dm, wide), BF),
-            sds((dm, half), BF),
+            sds(terms, BF),
             sds((dm, half), BF),
             sds(terms, BF),
             sds((8, dm), F32),
@@ -771,11 +810,12 @@
             v((rows, dm), F32),
             v((seqs, wide // HD, full, HD), BF),
             v(first, BF),
+            v(first, BF),
             dma((3, 4)),
             dma((2,)),
-            dma((4,)),
-            dma((3, seqs, 4, nt)),
-            dma((3, seqs, 6, 2 * nt - 1)),
+            dma((2, 4)),
+            dma((3, seqs, SPLIT, 4, nt)),
+            dma((3, seqs, SPLIT, 6, 2 * nt - 1)),
             dma((seqs, wide // HD, 2)),
             dma((seqs,)),
             dma((4,)),
@@ -986,7 +1026,7 @@
     ws[3].relay()
     ws[4].relay()
 
-    for s in range(seqs):
+    def attend(s):
         for k in (2, 0, 1):
             wait_bytes(qkvh.at[k, s], hrecv.at[k, s])
         for i in range(e.nc):
@@ -1003,6 +1043,8 @@
             atth[s, i] = dot(probs, vb, NN).astype(BF)
         dst = att.at[s, own, cut(lax.rem(e.c, heads), HD)]
         from_heads(e, atth.at[s], dst, bsend.at[s], brecv.at[s], heads)
+
+    loop(seqs, attend)
     for k, (a, b) in enumerate(((qkvh, qkv_heads), (atth, att_heads))):
         outs.append(pltpu.make_async_copy(a, b, osem.at[4 + k]))
         outs[-1].start()
@@ -1042,7 +1084,7 @@
             sds((dm, wide), BF),
             sds((dm, wide), BF),
             sds((dm, wide), BF),
-            sds((dm, gate.shape[1] // 4), BF),
+            sds((dm, gate.shape[1] // 8), BF),
             sds((2, seqs, full, wide), F32),
             sds((seqs, full, 128), F32),
             sds((2, seqs, full, HD), F32),
@@ -1085,10 +1127,10 @@
     sizes, seqs, rows,
     hidden_grad, gains_in, units, scales, angles, qgain, kgain, seg_col, seg_row, lse,
     agh_in, qkv_heads, att_heads, xs_in, wq_in, wk_in, wv_in,
-    wo_part, gate_part, up_part,
-    input_grad, gains_out, in_q, in_k, in_v, in_o, in_g, in_u,
+    wo_part, up_part,
+    input_grad, gains_out, in_q, in_k, in_v, in_o, in_u,
     agh, qkvh, atth, x, wq, wk, wv, dh, dx, acck, accv, uu, pre, part, pair, right, left, y,
-    mine, inbox, wide_t, gmine, gin, gin2, p_o, p_g, p_u, f_q, f_k, f_v, f_o, f_g, f_u,
+    mine, inbox, wide_t, gmine, gin, gin2, p_o, p_u, f_q, f_k, f_v, f_o, f_u,
     lsem, dsend, drecv, esem, rsem, ssem, g1sem, g2sem,
 ):
     e = Place(*sizes)
@@ -1102,7 +1144,7 @@
         for k, (p, fi, b) in enumerate(
             (
                 (wq, f_q, in_q), (wk, f_k, in_k), (wv, f_v, in_v),
-                (p_o, f_o, in_o), (p_g, f_g, in_g), (p_u, f_u, in_u),
+                (p_o, f_o, in_o), (p_u, f_u, in_u),
             )
         )
     ]
@@ -1112,7 +1154,7 @@
             (
                 (qkv_heads, qkvh), (agh_in, agh), (att_heads, atth), (wq_in, wq),
                 (wk_in, wk), (wv_in, wv), (xs_in, x),
-                (gate_part, p_g), (wo_part, p_o), (up_part, p_u),
+                (up_part, p_u), (wo_part, p_o),
             )
         )
     ]
@@ -1127,7 +1169,7 @@
     for ld in loads[:3]:
         ld.wait()
 
-    for s in range(seqs):
+    def attend_back(s):
         acck[...] = jnp.zeros_like(acck)
         accv[...] = jnp.zeros_like(accv)
         for i in range(e.nc):
@@ -1150,10 +1192,10 @@
         for k in range(3):
             dst = dx.at[k, s, lax.rem(e.c, heads), own, :]
             from_heads(e, dh.at[k, s], dst, dsend.at[k, s], drecv.at[k, s], heads)
+
+    loop(seqs, attend_back)
     scat[4].relay()
     scat[3].relay()
-    loads[9].wait()
-    scat[5].start()
 
     place = cut(e.t * 2 + e.p, wide)
     gmine[...] = gains_in[...]
@@ -1216,18 +1258,16 @@
 
         loop(dm // tile, step)
         scat[k].start()
-        for s in range(seqs):
-            red[s].slot(k)
-        if k == 0:
-            scat[5].relay()
-    for j in range(3, n - 1):
+    for j in range(n - 1):
+        if j == n - 2:
+            scat[0].relay()
+            scat[1].relay()
         for s in range(seqs):
             red[s].slot(j)
+    scat[2].relay()
     gmine[...] = gx.finish()
     gx2 = Exchange(e, gmine, gin2, g2sem.at[0], g2sem.at[1], *Exchange.line(e))
     gx2.start()
-    for k in range(3):
-        scat[k].relay()
     for s in range(seqs):
         red[s].result(y)
         input_grad[s] = hidden_grad[s] + y[...]
@@ -1243,9 +1283,9 @@
 
 def tail_stage(sizes, *args):
     nf, nc, nt = sizes
-    hidden_grad, xs, gate_part, wo_part = args[0], args[13], args[18], args[17]
+    hidden_grad, up_part, wo_part = args[0], args[18], args[17]
     seqs, rows, dm = hidden_grad.shape
-    half, wide = gate_part.shape[1], wo_part.shape[1]
+    half, wide = up_part.shape[1], wo_part.shape[1]
     heads = wide // HD
     full = 2 * nt * rows
     span = nt * rows
@@ -1258,9 +1298,9 @@
         name="tail_stage",
         out_shape=(sds((seqs, rows, dm), F32), sds((8, dm), F32))
         + (sds(small_terms, BF),) * 4
-        + (sds(large_terms, BF),) * 2,
-        in_specs=[VMEM_SPEC] * 10 + [HBM_SPEC] * 10,
-        out_specs=(VMEM_SPEC,) * 2 + (HBM_SPEC,) * 6,
+        + (sds(large_terms, BF),),
+        in_specs=[VMEM_SPEC] * 10 + [HBM_SPEC] * 9,
+        out_specs=(VMEM_SPEC,) * 2 + (HBM_SPEC,) * 5,
         scratch_shapes=[
             v((seqs, nc, span, HD), BF),
             v((3, seqs, nc, span, HD), BF),
@@ -1288,19 +1328,17 @@
             v((nt, 8, dm), F32),
             v((dm, wide), BF),
             v((dm, half), BF),
-            v((dm, half), BF),
             v(small, BF),
             v(small, BF),
             v(small, BF),
             v(small, BF),
             v(large, BF),
-            v(large, BF),
-            dma((10,)),
+            dma((9,)),
             dma((3, seqs, nc)),
             dma((3, seqs)),
             dma((2, 2 * nt)),
             dma((seqs, 4, nt)),
-            dma((6, 4)),
+            dma((5, 4)),
             dma((2, nf * nc)),
             dma((2, nt)),
         ],
@@ -1308,6 +1346,32 @@
             collective_id=3, has_side_effects=True, vmem_limit_bytes=63 << 20
         ),
     )(*args)
+
+
+def add_kernel(count, *refs):
+    for src, dst in zip(refs[:count], refs[count:]):
+        total = src[0].astype(F32)
+        for i in range(1, src.shape[0]):
+            total += src[i].astype(F32)
+        dst[...] = total
+
+
+def add_terms(terms):
+    steps = 4
+
+    def rows(x):
+        return x.shape[1] // steps
+
+    return pl.pallas_call(
+        functools.partial(add_kernel, len(terms)),
+        name="add_terms",
+        grid=(steps,),
+        out_shape=tuple(jax.ShapeDtypeStruct(x.shape[1:], F32) for x in terms),
+        in_specs=[
+            pl.BlockSpec((x.shape[0], rows(x), x.shape[2]), lambda i: (0, i, 0)) for x in terms
+        ],
+        out_specs=tuple(pl.BlockSpec((rows(x), x.shape[2]), lambda i: (i, 0)) for x in terms),
+    )(*terms)
 
 
 def body(
@@ -1331,15 +1395,15 @@
         sizes, tokens, cos_own, sin_own, qgain, kgain, seg_col, seg_row,
         query_weight, key_weight, value_weight, output_weight, gate_weight,
     )
-    block_out, hidden_grad, agh, wo_part, gate_part, up_part, down_terms, gains = ffn_stage(
+    block_out, hidden_grad, agh, wo_part, gate_terms, up_part, down_terms, gains = ffn_stage(
         sizes, att, wo, gate, gate_weight, up_projection_weight, down_weight,
         tokens, cotangent, attention_gain[None], feedforward_gain[None],
     )
-    input_grad, gain_sums, *terms = tail_stage(
+    input_grad, gain_sums, *terms, up_terms = tail_stage(
         sizes, hidden_grad, gains, units, scales, angles, qgain, kgain, seg_col, seg_row, lse,
-        agh, qkv_heads, att_heads, xs, wq, wk, wv, wo_part, gate_part, up_part,
+        agh, qkv_heads, att_heads, xs, wq, wk, wv, wo_part, up_part,
     )
-    weight_grads = [jnp.sum(x.astype(F32), axis=0) for x in (*terms, down_terms)]
+    weight_grads = add_terms((*terms, gate_terms, up_terms, down_terms))
     return (block_out, input_grad, *weight_grads, *(gain_sums[k] for k in range(4)))
 
 

time: 505 us -> 496 us (0.982)
  other arithmetic: 13.8 us -> 2.69 us
    pallas_call x1, Pallas kernels: 250 us -> 275 us  [ffn_stage(): pl.pallas_call(functools.partial(ffn_kernel, sizes, seqs, rows), name='ff...]
    pallas_call x1, Pallas kernels: 136 us -> 113 us  [tail_stage(): pl.pallas_call(functools.partial(tail_kernel, sizes, seqs, rows), name='t...]
    reduce_sum x7 -> x0, other arithmetic: 11.1 us -> none  [body(): jnp.sum(x.astype(F32), axis=0)]
    pallas_call x1, Pallas kernels: 91.9 us -> 83.4 us  [front_stage(): pl.pallas_call(functools.partial(front_kernel, sizes, seqs, rows), name='...]
    pallas_call x0 -> x1, Pallas kernels: none -> 7.15 us  [add_terms(): pl.pallas_call(functools.partial(add_kernel, len(terms)), name='add_terms...]
where the time goes in v3:
time: 496 us; the launch traced here: 488 us
  Pallas kernels  478 us (96%)
  local copies, waits for them, and re-layouts  6.04 us (1%)
    pallas_call x1, Pallas kernels, ffn_stage(): pl.pallas_call(functools.partial(ffn_kernel, sizes, seqs, rows), name='ff...  275 us
    pallas_call x1, Pallas kernels, tail_stage(): pl.pallas_call(functools.partial(tail_kernel, sizes, seqs, rows), name='t...  113 us
    pallas_call x1, Pallas kernels, front_stage(): pl.pallas_call(functools.partial(front_kernel, sizes, seqs, rows), name='...  83.4 us

profile of v3, /device:TPU:0, one launch (start us, length us, event | category | flops | bytes accessed | tf_op | source)
XLA Modules:
  0.0 487.7 jit_solution(1599033279094837772)
XLA Ops:
  0.6 0.0 copy-start.2
  0.7 0.7 dynamic-slice_convert_fusion
  1.4 1.3 broadcast_in_dim.23.seg_row
  2.7 1.0 fusion
  3.7 1.0 pad_maximum_fusion
  4.7 0.0 copy-done.2
  4.7 1.3 copy.28.seg_col
  6.0 83.4 %front_stage.1 = (bf16[2,512,256]{2,1,0:T(8,128)(2,1)}, bf16[2,512,2048]{2,1,0:T(8,128)(2,1)}, bf16[2048,256]{1,0:T(8,128)(2,1)}, bf16[2048,256]{1,0:T(8,128)(2,...) custom-call(bf16[2,64,2048]{2,1,0:T(8,128)(2,1)} %tokens.3, ...), custom_call_target="tpu_custom_call" | custom-call | tf_op jit(solution)/shard_map/front_stage/pallas_call | solution.py:1077
  89.4 274.8 %ffn_stage.1 = (bf16[2,64,2048]{2,1,0:T(8,128)(2,1)}, f32[2,64,2048]{2,1,0:T(8,128)}, bf16[2,4,256,128]{3,2,1,0:T(8,128)(2,1)}, bf16[2048,256]{1,0:T(8,128)(2,1)...) custom-call(bf16[2,512,256]{2,1,0:T(8,128)(2,1)} %get-tuple-element., ...), custom_call_target="tpu_custom_call" | custom-call | tf_op jit(solution)/shard_map/ffn_stage/pallas_call | solution.py:777
  364.2 112.7 %tail_stage.1 = (f32[2,64,2048]{2,1,0:T(8,128)}, f32[8,2048]{1,0:T(8,128)}, bf16[2,256,512]{2,1,0:T(8,128)(2,1)}, bf16[2,256,512]{2,1,0:T(8,128)(2,1)}, bf16[2,2...) custom-call(f32[2,64,2048]{2,1,0:T(8,128)} %get-tuple-element.52.hidden_grad, ...), custom_call_target="tpu_custom_call" | custom-call | tf_op jit(solution)/shard_map/tail_stage/pallas_call | solution.py:1296
  476.9 1.6 fusion.1
  478.5 0.0 copy-start.1
  478.5 0.0 copy-start
  478.5 7.2 %add_terms.1 = (f32[256,512]{1,0:T(8,128)}, f32[256,512]{1,0:T(8,128)}, f32[256,512]{1,0:T(8,128)}, f32[256,512]{1,0:T(8,128)}, f32[256,2048]{1,0:T(8,128)}, /*index=5*/f32[256,2048]{1,0:T(8,128)}, f32[256,2048]{1,0:T(8,128)}) custom-call(bf16[2,256,512]{2,1,0:T(8,128)(2,1)} %get-tuple-element.68.refs_0_, bf16[2,256,512]{2,1,0:T(8,128)(2,1)} %get-tuple-element.69.refs_1_, ...), custom_call_target="tpu_custom_call" | custom-call | tf_op jit(solution)/shard_map/add_terms/pallas_call | solution.py:1365
  485.7 0.0 copy-done.1
  485.7 0.8 copy.32
  486.5 0.0 copy-done
  486.5 1.0 copy.33
  (1 shorter events, 0.0 us)
Async XLA Ops:
  0.6 4.0 copy-start.2
  478.5 7.2 %copy-start.1 = (bf16[2,64,2048]{2,1,0:T(8,128)(2,1)S(1)}, bf16[2,64,2048]{2,1,0:T(8,128)(2,1)}, u32[]{:S(2)}) copy-start(bf16[2,64,2048]{2,1,0:T(8,128)(2,1)} %get-tuple-element.105) | copy-start | bytes 1572868
  478.5 8.0 %copy-start = (f32[2,64,2048]{2,1,0:T(8,128)S(1)}, f32[2,64,2048]{2,1,0:T(8,128)}, u32[]{:S(2)}) copy-start(f32[2,64,2048]{2,1,0:T(8,128)} %get-tuple-element.106) | copy-start | bytes 3145732

commit v4 on v3

--- a/solution.py
+++ b/solution.py
@@ -1161,8 +1161,6 @@
     for ld in loads:
         ld.start()
     e.barrier()
-    loads[7].wait()
-    scat[4].start()
     loads[8].wait()
     scat[3].start()
     wide_t[...] = jnp.zeros_like(wide_t)
@@ -1194,7 +1192,8 @@
             from_heads(e, dh.at[k, s], dst, dsend.at[k, s], drecv.at[k, s], heads)
 
     loop(seqs, attend_back)
-    scat[4].relay()
+    loads[7].wait()
+    scat[4].start()
     scat[3].relay()
 
     place = cut(e.t * 2 + e.p, wide)
@@ -1234,7 +1233,13 @@
 
     tile = 512
     red = [
-        Reduce(e, part.at[s], pair.at[s], right.at[s], left.at[s], rsem.at[s], rows)
+        Both(
+            Reduce(
+                e, part.at[s, :, cl], pair.at[s, :, cl], right.at[s, :, :, cl],
+                left.at[s, :, :, cl], rsem.at[s, u], rows,
+            )
+            for u, cl in enumerate(parts_of(dm))
+        )
         for s in range(seqs)
     ]
     for s in range(seqs):
@@ -1258,6 +1263,7 @@
 
         loop(dm // tile, step)
         scat[k].start()
+    scat[4].relay()
     for j in range(n - 1):
         if j == n - 2:
             scat[0].relay()
@@ -1269,7 +1275,8 @@
     gx2 = Exchange(e, gmine, gin2, g2sem.at[0], g2sem.at[1], *Exchange.line(e))
     gx2.start()
     for s in range(seqs):
-        red[s].result(y)
+        for r, cl in zip(red[s].each, parts_of(dm)):
+            r.result(y.at[:, cl])
         input_grad[s] = hidden_grad[s] + y[...]
     gains_out[...] = gx2.finish()
     for sc in scat:
@@ -1337,7 +1344,7 @@
             dma((3, seqs, nc)),
             dma((3, seqs)),
             dma((2, 2 * nt)),
-            dma((seqs, 4, nt)),
+            dma((seqs, SPLIT, 4, nt)),
             dma((5, 4)),
             dma((2, nf * nc)),
             dma((2, nt)),

time: 496 us -> 486 us (0.980)
  Pallas kernels: 478 us -> 468 us
    pallas_call x1, Pallas kernels: 113 us -> 102 us  [tail_stage(): pl.pallas_call(functools.partial(tail_kernel, sizes, seqs, rows), name='t...]
where the time goes in v4:
time: 486 us; the launch traced here: 477 us
  Pallas kernels  468 us (96%)
  local copies, waits for them, and re-layouts  6.04 us (1%)
    pallas_call x1, Pallas kernels, ffn_stage(): pl.pallas_call(functools.partial(ffn_kernel, sizes, seqs, rows), name='ff...  275 us
    pallas_call x1, Pallas kernels, tail_stage(): pl.pallas_call(functools.partial(tail_kernel, sizes, seqs, rows), name='t...  102 us
    pallas_call x1, Pallas kernels, front_stage(): pl.pallas_call(functools.partial(front_kernel, sizes, seqs, rows), name='...  83.4 us

profile of v4, /device:TPU:0, one launch (start us, length us, event | category | flops | bytes accessed | tf_op | source)
XLA Modules:
  0.0 477.4 jit_solution(5527889837245565464)
XLA Ops:
  0.6 0.0 copy-start.2
  0.7 0.7 dynamic-slice_convert_fusion
  1.4 1.3 broadcast_in_dim.23.seg_row
  2.7 1.0 fusion
  3.7 1.0 pad_maximum_fusion
  4.7 0.0 copy-done.2
  4.7 1.3 copy.28.seg_col
  6.0 83.4 %front_stage.1 = (bf16[2,512,256]{2,1,0:T(8,128)(2,1)}, bf16[2,512,2048]{2,1,0:T(8,128)(2,1)}, bf16[2048,256]{1,0:T(8,128)(2,1)}, bf16[2048,256]{1,0:T(8,128)(2,...) custom-call(bf16[2,64,2048]{2,1,0:T(8,128)(2,1)} %tokens.3, ...), custom_call_target="tpu_custom_call" | custom-call | tf_op jit(solution)/shard_map/front_stage/pallas_call | solution.py:1077
  89.4 274.8 %ffn_stage.1 = (bf16[2,64,2048]{2,1,0:T(8,128)(2,1)}, f32[2,64,2048]{2,1,0:T(8,128)}, bf16[2,4,256,128]{3,2,1,0:T(8,128)(2,1)}, bf16[2048,256]{1,0:T(8,128)(2,1)...) custom-call(bf16[2,512,256]{2,1,0:T(8,128)(2,1)} %get-tuple-element., ...), custom_call_target="tpu_custom_call" | custom-call | tf_op jit(solution)/shard_map/ffn_stage/pallas_call | solution.py:777
  364.2 102.5 %tail_stage.1 = (f32[2,64,2048]{2,1,0:T(8,128)}, f32[8,2048]{1,0:T(8,128)}, bf16[2,256,512]{2,1,0:T(8,128)(2,1)}, bf16[2,256,512]{2,1,0:T(8,128)(2,1)}, bf16[2,2...) custom-call(f32[2,64,2048]{2,1,0:T(8,128)} %get-tuple-element.52.hidden_grad, ...), custom_call_target="tpu_custom_call" | custom-call | tf_op jit(solution)/shard_map/tail_stage/pallas_call | solution.py:1303
  466.6 1.6 fusion.1
  468.3 0.0 copy-start.1
  468.3 0.0 copy-start
  468.3 7.2 %add_terms.1 = (f32[256,512]{1,0:T(8,128)}, f32[256,512]{1,0:T(8,128)}, f32[256,512]{1,0:T(8,128)}, f32[256,512]{1,0:T(8,128)}, f32[256,2048]{1,0:T(8,128)}, /*index=5*/f32[256,2048]{1,0:T(8,128)}, f32[256,2048]{1,0:T(8,128)}) custom-call(bf16[2,256,512]{2,1,0:T(8,128)(2,1)} %get-tuple-element.68.refs_0_, bf16[2,256,512]{2,1,0:T(8,128)(2,1)} %get-tuple-element.69.refs_1_, ...), custom_call_target="tpu_custom_call" | custom-call | tf_op jit(solution)/shard_map/add_terms/pallas_call | solution.py:1372
  475.4 0.0 copy-done.1
  475.4 0.8 copy.32
  476.2 0.0 copy-done
  476.2 1.0 copy.33
  (1 shorter events, 0.0 us)
Async XLA Ops:
  0.6 4.0 copy-start.2
  468.3 7.2 %copy-start.1 = (bf16[2,64,2048]{2,1,0:T(8,128)(2,1)S(1)}, bf16[2,64,2048]{2,1,0:T(8,128)(2,1)}, u32[]{:S(2)}) copy-start(bf16[2,64,2048]{2,1,0:T(8,128)(2,1)} %get-tuple-element.105) | copy-start | bytes 1572868
  468.3 8.0 %copy-start = (f32[2,64,2048]{2,1,0:T(8,128)S(1)}, f32[2,64,2048]{2,1,0:T(8,128)}, u32[]{:S(2)}) copy-start(f32[2,64,2048]{2,1,0:T(8,128)} %get-tuple-element.106) | copy-start | bytes 3145732
